TPU v7x, 256 devices: a whole 4x4x8 slice. The times are simulated.
256 devices in a mesh: gx: 16 (over y, x), gy: 16 (over z, core).
Axes of the slice: x: 4, y: 4, z: 8, core: 2. Of those that a mesh axis runs over, the one named last changes fastest.
Arguments:
- background: bfloat16 [40, 256, 512, 128], P(None, 'gx', 'gy'), may hold values from -6 to 6
- obs_perturb: bfloat16 [16, 16, 40, 256], P('gx', 'gy'), may hold values from -1.796875 to 1.796875
- innovation: float32 [16, 16, 256], P('gx', 'gy'), may hold values from -3.8 to 3.8
- obs_precision: float32 [16, 16, 256], P('gx', 'gy'), may hold values from 0.3 to 3
- obs_column: int32 [16, 16, 256], P('gx', 'gy'), may hold values from 0 to 511
- obs_count: int32 [16, 16], P('gx', 'gy'), may hold values from 64 to 256, as said below
Outputs:
- analysis: bfloat16 [40, 256, 512, 128], P(None, 'gx', 'gy')
Inputs may be any that keep to these rules, and one draw needn't show every extreme that they name: Slots 0 to obs_count - 1 of a tile hold observations, the others are padding; in every draw some tile has all 256 slots live.
All inputs are finite; a program needn't handle non-finite values.
Results may differ from a plain program's by a relative error of at most 0.001.
Values sent between devices are 32-bit elements; how exact they have to be, the bound alone decides.
A program may use at most 128 MiB of HBM per device.

v0:
```python
import math

import jax
import jax.numpy as jnp
from jax import lax
from jax.sharding import Mesh
from jax.sharding import PartitionSpec as P

SPAN = 2
GX = ("gx_0", "gx_1")
GY = ("gy_0", "gy_1")
GX_GY = ("gx_0", "gx_1", "gy_0", "gy_1")


def one_axis_at_a_time(value, axes):
    for axis in axes:
        value = lax.psum(value, axis)
    return value


def with_halo(cells, sides, width):
    for axis, dim in sides:
        count = lax.axis_size(axis)
        head = lax.slice_in_dim(cells, 0, width, axis=dim)
        tail = lax.slice_in_dim(cells, cells.shape[dim] - width, cells.shape[dim], axis=dim)
        cells = jnp.concatenate(
            [
                lax.ppermute(tail, axis, [(i, (i + 1) % count) for i in range(count)]),
                cells,
                lax.ppermute(head, axis, [((i + 1) % count, i) for i in range(count)]),
            ],
            axis=dim,
        )
    return cells


def pair_table(centered, values):
    members = centered.shape[0]
    squares = (centered[:, None, :] * centered[None, :, :]).reshape(
        members * members, centered.shape[1]
    )
    return jnp.concatenate([squares, centered * values[None, :]], axis=0)


def taper(east_pos, north_pos, centre_east, centre_north, period, radius):
    offset_east = (
        jnp.mod(east_pos[:, None] - centre_east[None, :] + 0.5 * period, period) - 0.5 * period
    )
    offset_north = north_pos[:, None] - centre_north[None, :]
    ratio = (offset_east * offset_east + offset_north * offset_north) / (radius * radius)
    return jnp.square(jnp.maximum(1.0 - ratio, 0.0))


def region_centres(
    tile_east, northward_tile, count_east, count_north, span, width_east, width_north
):
    rows_east = (jnp.arange(count_east) * span).astype(jnp.float32) + 0.5 * span
    rows_north = (jnp.arange(count_north) * span).astype(jnp.float32) + 0.5 * span
    base_east = (tile_east * width_east).astype(jnp.float32)
    base_north = (northward_tile * width_north).astype(jnp.float32)
    centre_east = jnp.broadcast_to(
        base_east + rows_east[:, None], (count_east, count_north)
    ).reshape(-1)
    centre_north = jnp.broadcast_to(
        base_north + rows_north[None, :], (count_east, count_north)
    ).reshape(-1)
    return (centre_east, centre_north)


def chol_lower(system):
    members = system.shape[0]
    rows = jnp.arange(members)
    remain = system
    columns = []
    for pivot_id in range(members):
        pivot = jnp.sqrt(remain[pivot_id, pivot_id])
        column = jnp.where((rows >= pivot_id)[:, None], remain[:, pivot_id] / pivot[None, :], 0.0)
        columns.append(column)
        remain = remain - column[:, None, :] * column[None, :, :]
    return jnp.stack(columns, axis=1)


def lower_inverse(factor):
    members = factor.shape[0]
    remain = jnp.broadcast_to(jnp.eye(members, dtype=factor.dtype)[:, :, None], factor.shape)
    solved = []
    for pivot_id in range(members):
        row_now = remain[pivot_id] / factor[pivot_id, pivot_id][None, :]
        solved.append(row_now)
        remain = remain - factor[:, pivot_id][:, None, :] * row_now[None, :, :]
    return jnp.stack(solved, axis=0)


def transform_of(gram, prior_term, members):
    square = members * members
    system = (
        gram[:square].reshape(members, members, -1)
        + prior_term * jnp.eye(members, dtype=gram.dtype)[:, :, None]
    )
    pull = gram[square:]
    inverse = lower_inverse(chol_lower(system))
    inner = jnp.einsum("imr,mr->ir", inverse, pull, precision=lax.Precision.HIGHEST)
    mean_weights = jnp.einsum("imr,ir->mr", inverse, inner, precision=lax.Precision.HIGHEST)
    return mean_weights[:, None, :] + math.sqrt(members - 1) * jnp.transpose(inverse, (1, 0, 2))


def interp_matrix(columns, regions, span):
    position = jnp.arange(columns).astype(jnp.float32) + 0.5
    centre = (jnp.arange(regions + 2) - 1).astype(jnp.float32) * span + 0.5 * span
    return jnp.maximum(1.0 - jnp.abs(position[:, None] - centre[None, :]) / span, 0.0)


def apply_tile(state_tile, local_frame, span):
    members, cols_east, cols_north, levels = state_tile.shape
    interpolation_rows = interp_matrix(cols_east, local_frame.shape[0] - 2, span)
    interp_cols = interp_matrix(cols_north, local_frame.shape[1] - 2, span)
    halfway_result = jnp.einsum(
        "br,rjg->bjg", interpolation_rows, local_frame, precision=lax.Precision.HIGHEST
    )
    column_transform = jnp.einsum(
        "bq,aqm->abm", interp_cols, halfway_result, precision=lax.Precision.HIGHEST
    )
    column_transform = column_transform.reshape(cols_east, cols_north, members, members)
    float_state = state_tile.astype(jnp.float32)
    centre_mean = jnp.mean(float_state, axis=0)
    spread = float_state - centre_mean[None]
    update = jnp.einsum(
        "jabl,abjk->kabl", spread, column_transform, precision=lax.Precision.HIGHEST
    )
    return (centre_mean[None] + update).astype(jnp.bfloat16)


def per_device(background, obs_perturb, innovation, obs_precision, obs_column, obs_count):
    members, cols_east, cols_north, levels = background.shape
    square = members * members
    regions_east = cols_east // SPAN
    regions_north = cols_north // SPAN
    count_east = lax.axis_size(GX)
    count_north = lax.axis_size(GY)
    tile_east = lax.axis_index(GX)
    northward_tile = lax.axis_index(GY)
    slot_count = obs_perturb.shape[3]
    centered = obs_perturb[0, 0].astype(jnp.float32)
    centered = centered - jnp.mean(centered, axis=0, keepdims=True)
    values = innovation[0, 0]
    slots = jnp.arange(slot_count, dtype=jnp.int32)
    weight = obs_precision[0, 0] * (slots < obs_count[0, 0]).astype(jnp.float32)
    column = obs_column[0, 0]
    east_pos = (tile_east * cols_east + column // cols_north).astype(jnp.float32) + 0.5
    north_pos = (northward_tile * cols_north + column % cols_north).astype(jnp.float32) + 0.5
    numer, denom = (
        one_axis_at_a_time(jnp.sum(weight * values * values), GX_GY),
        one_axis_at_a_time(
            jnp.sum(weight * jnp.sum(centered * centered, axis=0)) / (members - 1), GX_GY
        ),
    )
    prior_term = (members - 1) / (numer / denom)
    period = float(count_east * cols_east)
    radius = float(cols_east)
    bundle = jnp.concatenate(
        [centered, values[None], weight[None], east_pos[None], north_pos[None]], axis=0
    )
    nearby = with_halo(bundle[None, None], ((GX, 0), (GY, 1)), 1)
    centre_east, centre_north = region_centres(
        tile_east, northward_tile, regions_east, regions_north, SPAN, cols_east, cols_north
    )
    gram = jnp.zeros((square + members, regions_east * regions_north), jnp.float32)
    for place_east in range(3):
        for place_north in range(3):
            block_obs = nearby[place_east, place_north]
            products = pair_table(block_obs[:members], block_obs[members])
            reach = taper(
                block_obs[members + 2],
                block_obs[members + 3],
                centre_east,
                centre_north,
                period,
                radius,
            )
            reach = reach * block_obs[members + 1][:, None]
            gram = gram + jnp.dot(
                products, reach, precision=lax.Precision.HIGHEST, preferred_element_type=jnp.float32
            )
    trans = transform_of(gram, prior_term, members)
    grid = jnp.transpose(trans, (2, 0, 1)).reshape(regions_east, regions_north, square)
    rims = with_halo(grid, ((GX, 0), (GY, 1)), 1)
    first_row = jnp.where(northward_tile == 0, rims[:, 1:2], rims[:, 0:1])
    last_row = jnp.where(northward_tile == count_north - 1, rims[:, -2:-1], rims[:, -1:])
    local_frame = jnp.concatenate([first_row, rims[:, 1:-1], last_row], axis=1)
    return apply_tile(background, local_frame, float(SPAN))


def solution(mesh):
    finer = Mesh(mesh.devices.reshape(4, 4, 8, 2), ("gx_0", "gx_1", "gy_0", "gy_1"))
    return jax.shard_map(
        per_device,
        mesh=finer,
        in_specs=(
            P(None, GX, GY, None),
            P(GX, GY, None, None),
            P(GX, GY, None),
            P(GX, GY, None),
            P(GX, GY, None),
            P(GX, GY),
        ),
        out_specs=P(None, GX, GY, None),
        check_vma=False,
    )
```

profile of v0, /device:TPU:1, one launch (start us, length us, event | category | flops | bytes accessed | tf_op | source)
XLA Modules:
  0.0 180.6 jit_solution(13513791505612512157)
XLA Ops:
  4.3 5.8 %collective-permute-start.1 = (f32[1,1,44,256]{3,2,1,0:T(8,128)S(1)}, f32[1,1,44,256]{3,2,1,0:T(8,128)S(1)}, u32[]{:S(2)}, u32[]{:S(2)}) collective-permute-start(f32[1,1,44,256]{3,2,1,0:T(8,128)S(1)} %bitcast.666), channel_id=1, source_target_pairs={{16,0},{32,16},{48,32},{64,48},{80,64},{96,80},{112,96},{128,112},... | collective-permute-start | bytes 135176 | tf_op jit(solution)/shard_map/ppermute | solution.py:30
  12.0 7.2 %all-reduce.2 = (f32[]{:T(128)}, f32[]{:T(128)}) all-reduce(f32[]{:T(128)S(6)} %div.1223, f32[]{:T(128)} %get-tuple-element.5), channel_id=1, replica_groups=mesh['gx_0'=4,'gx_1'=4,'gy_0'=8,'gy_1'=2] {'gx_0'}, use_global_device_ids=true, to_apply=%region_4.5 | all-reduce | flops 2 | bytes 16 | tf_op jit(solution)/shard_map/psum | solution.py:17
  19.3 11.0 %all-reduce.1 = (f32[]{:T(128)}, f32[]{:T(128)}) all-reduce(f32[]{:T(128)} %get-tuple-element.11, f32[]{:T(128)} %get-tuple-element.12), channel_id=1, replica_groups=mesh['gx_0'=4,'gx_1'=4,'gy_0'=8,'gy_1'=2] {'gx_1'}, use_global_device_ids=true, to_apply=%region_5.6 | all-reduce | flops 2 | bytes 16 | tf_op jit(solution)/shard_map/psum | solution.py:17
  30.3 16.9 %all-reduce = (f32[]{:T(128)}, f32[]{:T(128)}) all-reduce(f32[]{:T(128)} %get-tuple-element.9, f32[]{:T(128)} %get-tuple-element.10), channel_id=1, replica_groups=mesh['gx_0'=4,'gx_1'=4,'gy_0'=8,'gy_1'=2] {'gy_0'}, use_global_device_ids=true, to_apply=%region_6.7 | all-reduce | flops 2 | bytes 16 | tf_op jit(solution)/shard_map/psum | solution.py:17
  47.2 12.2 %all-reduce.3 = (f32[]{:T(128)}, f32[]{:T(128)}) all-reduce(f32[]{:T(128)} %get-tuple-element.7, f32[]{:T(128)} %get-tuple-element.8), channel_id=1, replica_groups=mesh['gx_0'=4,'gx_1'=4,'gy_0'=8,'gy_1'=2] {'gy_1'}, use_global_device_ids=true, to_apply=%region_7.8 | all-reduce | flops 2 | bytes 16 | tf_op jit(solution)/shard_map/psum | solution.py:17
  60.7 3.4 %convert_reduce_fusion = f32[16,32,128]{2,1,0:T(8,128)S(1)} fusion(bf16[40,16,32,128]{3,2,1,0:T(8,128)(2,1)} %param.6), kind=kLoop, calls=%fused_computation.1 | loop fusion | flops 5177344 | bytes 5505024 | tf_op jit(solution)/shard_map/reduce_sum | solution.py:125
  64.7 5.5 %convert_subtract_fusion = f32[40,16,32,128]{3,2,1,0:T(8,128)} fusion(bf16[40,16,32,128]{3,2,1,0:T(8,128)(2,1)S(1)} %copy-done, f32[16,32,128]{2,1,0:T(8,128)S(1)} %broadcast_multiply_fusion.9), kind=kLoop, calls=%fused_computation | loop fusion | flops 5242880 | bytes 15990784 | tf_op jit(solution)/shard_map/sub | solution.py:126
  73.1 1.7 fusion.19
  76.7 1.7 convolution_add_fusion.7
  78.4 1.7 convolution_add_fusion.6
  80.0 1.7 convolution_add_fusion.5
  83.4 1.9 %convolution_add_fusion.3 = f32[1640,128]{1,0:T(8,128)S(1)} fusion(f32[1640,128]{1,0:T(8,128)S(1)} %convolution_add_fusion.4, f32[40,256]{1,0:T(8,128)S(1)} %get-tuple-element.38, f32[1600,256]{1,0:T(8,128)S(1)} %bitcast.609, f32[256]{0:T(256)S(1)} %bitcast.741, f32[256]{0:T(256)S(1)} %bitcast.742, f32[256]{0:T(256)S(1)} %bitcast.743, f32[128]{0:T(128)S(1)} %sub.617, ...), kind=kOutput, calls=%fused_computation.11 | convolution fusion | flops 646093824 | bytes 3362816 | tf_op jit(solution)/shard_map/dot_general | solution.py:181
  85.2 1.7 convolution_add_fusion.2
  86.9 1.7 convolution_add_fusion.1
  115.9 5.2 %collective-permute-start.5 = (f32[1,16,1600]{2,0,1:T(1,128)}, f32[1,16,1600]{2,0,1:T(1,128)}, u32[]{:S(2)}, u32[]{:S(2)}) collective-permute-start(f32[1,16,1600]{2,0,1:T(1,128)} %slice.952), channel_id=1, source_target_pairs={{16,0},{32,16},{48,32},{64,48},{80,64},{96,80},{112,96},{128,112},... | collective-permute-start | bytes 307208 | tf_op jit(solution)/shard_map/ppermute | solution.py:30
  122.3 1.7 reshape.2960
  126.2 2.2 %collective-permute-start.6 = (f32[10,1,1600]{2,0,1:T(8,128)S(1)}, f32[10,1,1600]{2,0,1:T(8,128)S(1)}, u32[]{:S(2)}, u32[]{:S(2)}) collective-permute-start(f32[10,1,1600]{2,0,1:T(8,128)S(1)} %pad_maximum_fusion.1), channel_id=1, source_target_pairs={{0,1},{1,2},{2,3},{3,4},{4,5},{5,6},{6,7},{7,8},{8,9},{9,10},{10,1... | collective-permute-start | bytes 192008 | tf_op jit(solution)/shard_map/ppermute | solution.py:28
  128.3 1.7 collective-permute-done.6
  130.8 3.5 %collective-permute-start.7 = (f32[10,1,1600]{2,0,1:T(8,128)S(1)}, f32[10,1,1600]{2,0,1:T(8,128)S(1)}, u32[]{:S(2)}, u32[]{:S(2)}) collective-permute-start(f32[10,1,1600]{2,0,1:T(8,128)S(1)} %get-tuple-element.16), channel_id=1, source_target_pairs={{1,0},{2,1},{3,2},{4,3},{5,4},{6,5},{7,6},{8,7},{9,8},{10,9},{11,1... | collective-permute-start | bytes 192008 | tf_op jit(solution)/shard_map/ppermute | solution.py:30
  135.6 2.8 %fusion.6 = f32[16,18,1600]{2,0,1:T(8,128)S(1)} fusion(f32[10,1,1600]{2,0,1:T(8,128)S(1)} %broadcast_select_fusion, f32[1,16,1600]{2,0,1:T(1,128)} %collective-permute-done.5, f32[8,16,1600]{2,0,1:T(8,128)S(1)} %copy.140, f32[1,16,1600]{2,0,1:T(1,128)S(1)} %collective-permute-done.4, f32[10,1,1600]{2,0,1:T(8,128)S(1)} %get-tuple-element.15, ...), kind=kOutput, calls=%fused_computation.16 | convolution fusion | flops 56448800 | bytes 2995304 | tf_op jit(solution)/shard_map/br,rjg->bjg/dot_general | solution.py:117
  138.4 3.4 %convolution_bitcast_fusion = f32[16,32,1600]{2,1,0:T(8,128)S(1)} fusion(f32[16,18,1600]{2,0,1:T(8,128)S(1)} %fusion.6, f32[18]{0:T(128)S(1)} %multiply_add_fusion, f32[32]{0:T(128)S(1)} %convert_add_fusion.3), kind=kOutput, calls=%fused_computation.6 | convolution fusion | flops 176950080 | bytes 5120200 | tf_op jit(solution)/shard_map/bq,aqm->abm/dot_general | solution.py:120
  141.8 6.2 %reshape.2961 = f32[16,32,40,40]{3,2,1,0:T(8,128)} reshape(f32[16,32,1600]{2,1,0:T(8,128)S(1)} %convolution_bitcast_fusion) | data formatting | bytes 6553600 | tf_op jit(solution)/shard_map/reshape | solution.py:123
  148.0 28.8 %fusion.2 = bf16[40,16,32,128]{3,0,2,1:T(8,128)(2,1)S(1)} fusion(f32[16,32,128]{2,1,0:T(8,128)} %copy-done.1, f32[16,32,40,40]{3,2,1,0:T(8,128)} %reshape.2961, f32[40,16,32,128]{3,2,1,0:T(8,128)} %convert_subtract_fusion), kind=kOutput, calls=%fused_computation.5 | convolution fusion | flops 1263534080 | bytes 19267584 | tf_op jit(solution)/shard_map/jabl,abjk->kabl/dot_general | solution.py:127
  176.7 3.6 %copy.144 = bf16[40,16,32,128]{3,2,1,0:T(8,128)(2,1)} copy(bf16[40,16,32,128]{3,0,2,1:T(8,128)(2,1)S(1)} %fusion.2) | data formatting | bytes 10485760 | tf_op jit(solution)/shard_map/convert_element_type | solution.py:130
  (401 shorter events, 43.0 us)
Async XLA Ops:
  0.0 10.8 %copy-start.3 = (f32[1,1,256]{2,1,0:T(1,128)S(1)}, f32[1,1,256]{2,1,0:T(1,128)}, u32[]{:S(2)}) copy-start(f32[1,1,256]{2,1,0:T(1,128)} %param.9) | copy-start | bytes 3076
  0.0 10.8 %copy-start.2 = (f32[1,1,256]{2,1,0:T(1,128)S(1)}, f32[1,1,256]{2,1,0:T(1,128)}, u32[]{:S(2)}) copy-start(f32[1,1,256]{2,1,0:T(1,128)} %param.8) | copy-start | bytes 3076
  0.0 10.7 %copy-start.4 = (s32[1,1,256]{2,1,0:T(1,128)S(1)}, s32[1,1,256]{2,1,0:T(1,128)}, u32[]{:S(2)}) copy-start(s32[1,1,256]{2,1,0:T(1,128)} %param.10) | copy-start | bytes 3076
  4.3 66.8 %collective-permute-start.1 = (f32[1,1,44,256]{3,2,1,0:T(8,128)S(1)}, f32[1,1,44,256]{3,2,1,0:T(8,128)S(1)}, u32[]{:S(2)}, u32[]{:S(2)}) collective-permute-start(f32[1,1,44,256]{3,2,1,0:T(8,128)S(1)} %bitcast.666), channel_id=1, source_target_pairs={{16,0},{32,16},{48,32},{64,48},{80,64},{96,80},{112,96},{128,112},... | collective-permute-start | bytes 135176 | tf_op jit(solution)/shard_map/ppermute | solution.py:30
  10.1 61.0 %collective-permute-start = (f32[1,1,44,256]{3,2,1,0:T(8,128)S(1)}, f32[1,1,44,256]{3,2,1,0:T(8,128)S(1)}, u32[]{:S(2)}, u32[]{:S(2)}) collective-permute-start(f32[1,1,44,256]{3,2,1,0:T(8,128)S(1)} %bitcast.667), channel_id=1, source_target_pairs={{0,16},{16,32},{32,48},{48,64},{64,80},{80,96},{96,112},{112,128},... | collective-permute-start | bytes 135176 | tf_op jit(solution)/shard_map/ppermute | solution.py:28
  60.7 4.0 %copy-start = (bf16[40,16,32,128]{3,2,1,0:T(8,128)(2,1)S(1)}, bf16[40,16,32,128]{3,2,1,0:T(8,128)(2,1)}, u32[]{:S(2)}) copy-start(bf16[40,16,32,128]{3,2,1,0:T(8,128)(2,1)} %param.6) | copy-start | bytes 15728644
  64.7 5.5 %copy-start.1 = (f32[16,32,128]{2,1,0:T(8,128)}, f32[16,32,128]{2,1,0:T(8,128)S(1)}, u32[]{:S(2)}) copy-start(f32[16,32,128]{2,1,0:T(8,128)S(1)} %broadcast_multiply_fusion.9) | copy-start | bytes 786436
  71.1 4.9 %collective-permute-start.3 = (f32[3,1,44,256]{3,2,1,0:T(8,128)S(1)}, f32[3,1,44,256]{3,2,1,0:T(8,128)S(1)}, u32[]{:S(2)}, u32[]{:S(2)}) collective-permute-start(f32[3,1,44,256]{3,2,1,0:T(8,128)S(1)} %pad_maximum_fusion), channel_id=1, source_target_pairs={{1,0},{2,1},{3,2},{4,3},{5,4},{6,5},{7,6},{8,7},{9,8},{10,9},{11,1... | collective-permute-start | bytes 405512 | tf_op jit(solution)/shard_map/ppermute | solution.py:30
  71.5 3.5 %collective-permute-start.2 = (f32[3,1,44,256]{3,2,1,0:T(8,128)S(1)}, f32[3,1,44,256]{3,2,1,0:T(8,128)S(1)}, u32[]{:S(2)}, u32[]{:S(2)}) collective-permute-start(f32[3,1,44,256]{3,2,1,0:T(8,128)S(1)} %pad_maximum_fusion), channel_id=1, source_target_pairs={{0,1},{1,2},{2,3},{3,4},{4,5},{5,6},{6,7},{7,8},{8,9},{9,10},{10,1... | collective-permute-start | bytes 405512 | tf_op jit(solution)/shard_map/ppermute | solution.py:28
  114.7 10.8 %collective-permute-start.4 = (f32[1,16,1600]{2,0,1:T(1,128)}, f32[1,16,1600]{2,0,1:T(1,128)S(1)}, u32[]{:S(2)}, u32[]{:S(2)}) collective-permute-start(f32[1,16,1600]{2,0,1:T(1,128)} %slice.950), channel_id=1, source_target_pairs={{0,16},{16,32},{32,48},{48,64},{64,80},{80,96},{96,112},{112,128},... | collective-permute-start | bytes 307208 | tf_op jit(solution)/shard_map/ppermute | solution.py:28
  115.9 9.5 %collective-permute-start.5 = (f32[1,16,1600]{2,0,1:T(1,128)}, f32[1,16,1600]{2,0,1:T(1,128)}, u32[]{:S(2)}, u32[]{:S(2)}) collective-permute-start(f32[1,16,1600]{2,0,1:T(1,128)} %slice.952), channel_id=1, source_target_pairs={{16,0},{32,16},{48,32},{64,48},{80,64},{96,80},{112,96},{128,112},... | collective-permute-start | bytes 307208 | tf_op jit(solution)/shard_map/ppermute | solution.py:30
  126.2 3.9 %collective-permute-start.6 = (f32[10,1,1600]{2,0,1:T(8,128)S(1)}, f32[10,1,1600]{2,0,1:T(8,128)S(1)}, u32[]{:S(2)}, u32[]{:S(2)}) collective-permute-start(f32[10,1,1600]{2,0,1:T(8,128)S(1)} %pad_maximum_fusion.1), channel_id=1, source_target_pairs={{0,1},{1,2},{2,3},{3,4},{4,5},{5,6},{6,7},{7,8},{8,9},{9,10},{10,1... | collective-permute-start | bytes 192008 | tf_op jit(solution)/shard_map/ppermute | solution.py:28
  130.8 4.8 %collective-permute-start.7 = (f32[10,1,1600]{2,0,1:T(8,128)S(1)}, f32[10,1,1600]{2,0,1:T(8,128)S(1)}, u32[]{:S(2)}, u32[]{:S(2)}) collective-permute-start(f32[10,1,1600]{2,0,1:T(8,128)S(1)} %get-tuple-element.16), channel_id=1, source_target_pairs={{1,0},{2,1},{3,2},{4,3},{5,4},{6,5},{7,6},{8,7},{9,8},{10,9},{11,1... | collective-permute-start | bytes 192008 | tf_op jit(solution)/shard_map/ppermute | solution.py:30
where the time goes:
time: 183 us; the launch traced here: 181 us
  matrix products  50.1 us (27%)
  blocking collectives  47.3 us (26%)
  other arithmetic  36.2 us (20%)
  local copies, waits for them, and re-layouts  19.8 us (11%)
  starting transfers between devices  18.4 us (10%)
  between operations  4.73 us (3%)
  waiting for transfers between devices  4.06 us (2%)
    psum x4, blocking collectives, one_axis_at_a_time(): value = lax.psum(value, axis)  47.3 us
    dot_general x1, matrix products, apply_tile(): jnp.einsum('jabl,abjk->kabl', spread, column_transform, precision=lax.Pre...  28.8 us
    dot_general x9, matrix products, per_device(): jnp.dot(products, reach, precision=lax.Precision.HIGHEST, preferred_eleme...  15.1 us
    ppermute x4, starting transfers between devices, with_halo(): lax.ppermute(head, axis, [((i + 1) % count, i) for i in range(count)])  14.8 us
    sub x39, other arithmetic, chol_lower(): remain = remain - column[:, None, :] * column[None, :, :]  11.6 us
    reshape x1, local copies, waits for them, and re-layouts, apply_tile(): column_transform.reshape(cols_east, cols_north, members, members)  6.16 us
    sub x1, other arithmetic, apply_tile(): spread = float_state - centre_mean[None]  5.53 us
  transfers between devices with their start and end apart: 8, of which 4 were waited for; matrix products, arithmetic and copies ran while one was open for 10% of the time, Pallas kernels for 0%

commit v1 on v0

v1 whole, which is shorter than its diff:
```python
import functools
import math

import jax
import jax.numpy as jnp
from jax import lax
from jax.experimental import pallas as pl
from jax.experimental.pallas import tpu as pltpu
from jax.sharding import PartitionSpec as P

F32 = jnp.float32
BF16 = jnp.bfloat16
MESH = pl.DeviceIdType.MESH
NB = 16
M = 40
SLOTS = 256
CX, CY = 16, 32
RX, RY = 8, 16
NREG = RX * RY
ROWS = 48
GROUPS = 14
STRIDE = 40
NEIGHBOURS = [(-1, -1), (-1, 0), (-1, 1), (0, -1), (0, 1), (1, -1), (1, 0), (1, 1)]


def vmem_specs(count):
    return [pl.BlockSpec(memory_space=pltpu.VMEM)] * count


def exchange_kernel(
    obs_ref, innovation_ref, precision_ref, column_ref, count_ref,
    near_ref, total_ref,
    mine, landed, part_a, part_b, slots_a, slots_b,
    send_near, recv_near, send_a, recv_a, send_b, recv_b,
):
    gx = lax.axis_index("gx")
    gy = lax.axis_index("gy")

    def at(dx, dy):
        return (lax.rem(gx + dx + NB, NB), lax.rem(gy + dy + NB, NB))

    barrier = pltpu.get_barrier_semaphore()
    peers = [(0, d) for d in range(1, NB)] + [(d, 0) for d in range(1, NB)]
    peers += [(1, 1), (1, -1), (-1, 1), (-1, -1)]
    for dx, dy in peers:
        pl.semaphore_signal(barrier, inc=1, device_id=at(dx, dy), device_id_type=MESH)

    centered = obs_ref[...].astype(F32)
    centered = centered - jnp.sum(centered, axis=0, keepdims=True) * (1.0 / M)
    innovation = innovation_ref[...]
    slot = lax.broadcasted_iota(jnp.int32, (1, SLOTS), 1)
    weight = jnp.where(slot < count_ref[...], precision_ref[...], 0.0)
    column = column_ref[...]
    east = (gx * CX + lax.shift_right_logical(column, 5)).astype(F32) + 0.5
    north = (gy * CY + jnp.bitwise_and(column, 31)).astype(F32) + 0.5
    mine[0:M, :] = centered
    mine[M : M + 8, :] = jnp.concatenate(
        [innovation, weight, east, north, jnp.zeros((4, SLOTS), F32)], axis=0
    )
    numer = jnp.sum(weight * innovation * innovation, axis=1, keepdims=True)
    squares = jnp.sum(centered * centered, axis=0, keepdims=True)
    denom = jnp.sum(weight * squares, axis=1, keepdims=True) / (M - 1)
    lane = lax.broadcasted_iota(jnp.int32, (1, 128), 1)
    part = jnp.where(lane < 64, numer, denom)
    part_a[...] = part

    pl.semaphore_wait(barrier, len(peers))

    def spread(src, slots, send, recv, along_x):
        copies = []
        for d in range(1, NB):
            copy = pltpu.make_async_remote_copy(
                src_ref=src,
                dst_ref=slots.at[d],
                send_sem=send.at[d],
                recv_sem=recv.at[d],
                device_id=at(d, 0) if along_x else at(0, d),
                device_id_type=MESH,
            )
            copy.start()
            copies.append(copy)
        return copies

    first = spread(part_a, slots_a, send_a, recv_a, False)
    near = []
    for n, (dx, dy) in enumerate(NEIGHBOURS):
        copy = pltpu.make_async_remote_copy(
            src_ref=mine,
            dst_ref=landed.at[n],
            send_sem=send_near.at[n],
            recv_sem=recv_near.at[n],
            device_id=at(dx, dy),
            device_id_type=MESH,
        )
        copy.start()
        near.append(copy)
    for copy in first:
        copy.wait()
    for d in range(1, NB):
        part = part + slots_a[d]
    part_b[...] = part
    second = spread(part_b, slots_b, send_b, recv_b, True)
    near_ref[0] = mine[...]
    for n, copy in enumerate(near):
        copy.wait()
        near_ref[n + 1] = landed[n]
    for copy in second:
        copy.wait()
    for d in range(1, NB):
        part = part + slots_b[d]
    total_ref[...] = part


def exchange(obs, innovation, precision, column, count):
    return pl.pallas_call(
        exchange_kernel,
        out_shape=(
            jax.ShapeDtypeStruct((9, ROWS, SLOTS), F32),
            jax.ShapeDtypeStruct((1, 128), F32),
        ),
        in_specs=vmem_specs(5),
        out_specs=tuple(vmem_specs(2)),
        scratch_shapes=[
            pltpu.VMEM((ROWS, SLOTS), F32),
            pltpu.VMEM((8, ROWS, SLOTS), F32),
            pltpu.VMEM((1, 128), F32),
            pltpu.VMEM((1, 128), F32),
            pltpu.VMEM((NB, 1, 128), F32),
            pltpu.VMEM((NB, 1, 128), F32),
            pltpu.SemaphoreType.DMA((8,)),
            pltpu.SemaphoreType.DMA((8,)),
            pltpu.SemaphoreType.DMA((NB,)),
            pltpu.SemaphoreType.DMA((NB,)),
            pltpu.SemaphoreType.DMA((NB,)),
            pltpu.SemaphoreType.DMA((NB,)),
        ],
        compiler_params=pltpu.CompilerParams(collective_id=0, has_side_effects=True),
        name="exchange",
    )(obs, innovation, precision, column, count)


BLOCKS = [(ib, jb) for ib in range(5) for jb in range(ib, 5)]


def split(value):
    high = value.astype(BF16)
    return high, (value - high.astype(F32)).astype(BF16)


def solve_kernel(
    near_ref, total_ref, packed_ref, south_ref, north_ref, corner_ref,
    table_high, table_low, gram, upper, inverse, flat,
):
    gx = lax.axis_index("gx")
    gy = lax.axis_index("gy")
    region = lax.broadcasted_iota(jnp.int32, (NREG, SLOTS), 0)
    centre_east = (gx * CX + 2 * lax.shift_right_logical(region, 4)).astype(F32) + 1.0
    centre_north = (gy * CY + 2 * jnp.bitwise_and(region, 15)).astype(F32) + 1.0
    gram[...] = jnp.zeros_like(gram)
    table_high[...] = jnp.zeros_like(table_high)
    table_low[...] = jnp.zeros_like(table_low)

    def tile(t, carry):
        obs = near_ref.at[t]
        east = obs[M + 2 : M + 3, :]
        north = obs[M + 3 : M + 4, :]
        weight = obs[M + 1 : M + 2, :]
        innovation = obs[M : M + 1, :]
        de = east - centre_east + 128.0
        de = jnp.where(de < 0.0, de + 256.0, de)
        de = jnp.where(de >= 256.0, de - 256.0, de) - 128.0
        dn = north - centre_north
        reach = jnp.maximum(1.0 - (de * de + dn * dn) * (1.0 / 256.0), 0.0)
        reach = reach * reach * weight
        reach_high, reach_low = split(reach)
        both = jnp.concatenate([reach_high, reach_low], axis=0)
        for b, (ib, jb) in enumerate(BLOCKS):
            right = obs[8 * jb : 8 * jb + 8, :]
            for ii in range(0, 8, 2):
                i = 8 * ib + ii
                rows = jnp.concatenate(
                    [obs[i : i + 1, :] * right, obs[i + 1 : i + 2, :] * right], axis=0
                )
                high, low = split(rows)
                at = b * 64 + ii * 8
                table_high[at : at + 16, :] = high
                table_low[at : at + 16, :] = low
        pull = jnp.concatenate([obs[0:M, :] * innovation, jnp.zeros((8, SLOTS), F32)], axis=0)
        high, low = split(pull)
        table_high[960:1008, :] = high
        table_low[960:1008, :] = low
        for c in range(0, 1024, 256):
            total = None
            for table in (table_high, table_low):
                out = lax.dot_general(
                    table[c : c + 256, :], both, (((1,), (1,)), ((), ())),
                    preferred_element_type=F32,
                )
                out = out[:, :128] + out[:, 128:]
                total = out if total is None else total + out
            gram[c : c + 256, :] += total
        return carry

    lax.fori_loop(0, 9, tile, 0)

    lane = lax.broadcasted_iota(jnp.int32, (1, 128), 1)
    both = total_ref[...]
    numer = jnp.sum(jnp.where(lane == 0, both, 0.0), axis=1, keepdims=True)
    denom = jnp.sum(jnp.where(lane == 64, both, 0.0), axis=1, keepdims=True)
    prior = jnp.broadcast_to((M - 1) / (numer / denom), (8, 128))
    sub = lax.broadcasted_iota(jnp.int32, (8, 128), 0)
    inverse[...] = jnp.zeros_like(inverse)
    offset = {pair: 64 * b for b, pair in enumerate(BLOCKS)}

    for ib in range(5):
        cols = list(range(ib, 5))
        state = []
        for t in range(8):
            row = []
            for jb in cols:
                at = offset[(ib, jb)] + 8 * t
                value = gram[at : at + 8, :]
                if jb == ib:
                    value = value + jnp.where(sub == t, prior, 0.0)
                row.append(value)
            row += [jnp.zeros((8, 128), F32)] * ib
            state.append(row)

        def eliminate(p, state):
            base = p * M
            line = [upper[pl.ds(pl.multiple_of(base + 8 * jb, 8), 8), :] for jb in cols]
            line += [inverse[pl.ds(pl.multiple_of(base + 8 * jb, 8), 8), :] for jb in range(ib)]
            new = []
            for t in range(8):
                factor = upper[pl.ds(base + 8 * ib + t, 1), :]
                factor = jnp.broadcast_to(factor, (8, 128))
                new.append([s - factor * v for s, v in zip(state[t], line)])
            return new

        if ib:
            state = lax.fori_loop(0, 8 * ib, eliminate, state, unroll=4)
        state = [
            row + [jnp.where(sub == t, 1.0, 0.0).astype(F32)] for t, row in enumerate(state)
        ]
        for t in range(8):
            scale = lax.rsqrt(jnp.broadcast_to(state[t][0][t : t + 1, :], (8, 128)))
            state[t] = [v * scale for v in state[t]]
            for s in range(t + 1, 8):
                factor = jnp.broadcast_to(state[t][0][s : s + 1, :], (8, 128))
                state[s] = [a - factor * v for a, v in zip(state[s], state[t])]
            p = 8 * ib + t
            for jb, value in zip(cols, state[t][: len(cols)]):
                upper[p * M + 8 * jb : p * M + 8 * jb + 8, :] = value
            for jb, value in enumerate(state[t][len(cols) :]):
                inverse[p * M + 8 * jb : p * M + 8 * jb + 8, :] = value

    pull = [gram[960 + 8 * jb : 968 + 8 * jb, :] for jb in range(5)]
    mean = [jnp.zeros((8, 128), F32)] * 5
    sums = []
    for k in range(M):
        rows = [inverse[k * M + 8 * jb : k * M + 8 * jb + 8, :] for jb in range(k // 8 + 1)]
        inner = rows[0] * pull[0]
        plain = rows[0]
        for jb in range(1, len(rows)):
            inner = inner + rows[jb] * pull[jb]
            plain = plain + rows[jb]
        inner = jnp.broadcast_to(jnp.sum(inner, axis=0, keepdims=True), (8, 128))
        sums.append(jnp.broadcast_to(jnp.sum(plain, axis=0, keepdims=True), (8, 128)))
        for jb in range(len(rows)):
            mean[jb] = mean[jb] + rows[jb] * inner
    mean_sum = mean[0] + mean[1] + mean[2] + mean[3] + mean[4]
    mean_sum = jnp.broadcast_to(jnp.sum(mean_sum, axis=0, keepdims=True), (8, 128))
    root = math.sqrt(M - 1)
    for g in range(GROUPS):
        rows = []
        for part in range(3):
            k = part * GROUPS + g
            if k >= M:
                rows += [jnp.zeros((8, 128), F32)] * 5
                continue
            shift = (1.0 - mean_sum - root * sums[k]) * (1.0 / M)
            for jb in range(5):
                value = mean[jb] + shift
                if jb <= k // 8:
                    value = value + root * inverse[k * M + 8 * jb : k * M + 8 * jb + 8, :]
                rows.append(value)
        rows.append(jnp.zeros((8, 128), F32))
        turned = jnp.transpose(jnp.concatenate(rows, axis=0))
        packed_ref[g] = turned
        flat[g * NREG : (g + 1) * NREG, :] = turned
        south_ref[g] = flat[pl.ds(g * NREG, RX, stride=RY), :]
        north_ref[g] = flat[pl.ds(g * NREG + RY - 1, RX, stride=RY), :]
    flat[GROUPS * NREG : 16 * NREG, :] = jnp.zeros((2 * NREG, 128), F32)
    for c, r in enumerate((0, RY - 1, NREG - RY, NREG - 1)):
        corner_ref[c] = flat[pl.ds(r, 16, stride=NREG), :]


def solve(near, total):
    return pl.pallas_call(
        solve_kernel,
        out_shape=(
            jax.ShapeDtypeStruct((GROUPS, NREG, 128), F32),
            jax.ShapeDtypeStruct((GROUPS, RX, 128), F32),
            jax.ShapeDtypeStruct((GROUPS, RX, 128), F32),
            jax.ShapeDtypeStruct((4, 16, 128), F32),
        ),
        in_specs=vmem_specs(2),
        out_specs=tuple(vmem_specs(4)),
        scratch_shapes=[
            pltpu.VMEM((1024, SLOTS), BF16),
            pltpu.VMEM((1024, SLOTS), BF16),
            pltpu.VMEM((1024, NREG), F32),
            pltpu.VMEM((M * M, 128), F32),
            pltpu.VMEM((M * M, 128), F32),
            pltpu.VMEM((16 * NREG, 128), F32),
        ],
        name="solve",
    )(near, total)


def edge_kernel(
    packed_ref, south_ref, north_ref, corner_ref,
    west_out, east_out, south_out, north_out, corner_out,
    west, east, south, north, corner, send, recv,
):
    gx = lax.axis_index("gx")
    gy = lax.axis_index("gy")

    def at(dx, dy):
        return (lax.rem(gx + dx + NB, NB), lax.rem(gy + dy + NB, NB))

    barrier = pltpu.get_barrier_semaphore()
    for dx, dy in NEIGHBOURS:
        pl.semaphore_signal(barrier, inc=1, device_id=at(dx, dy), device_id_type=MESH)
    pl.semaphore_wait(barrier, len(NEIGHBOURS))
    plan = [
        (packed_ref.at[:, pl.ds(0, RY)], east, (-1, 0)),
        (packed_ref.at[:, pl.ds(NREG - RY, RY)], west, (1, 0)),
        (south_ref, north, (0, -1)),
        (north_ref, south, (0, 1)),
        (corner_ref.at[0], corner.at[3], (-1, -1)),
        (corner_ref.at[1], corner.at[2], (-1, 1)),
        (corner_ref.at[2], corner.at[1], (1, -1)),
        (corner_ref.at[3], corner.at[0], (1, 1)),
    ]
    copies = []
    for n, (src, dst, (dx, dy)) in enumerate(plan):
        copy = pltpu.make_async_remote_copy(
            src_ref=src,
            dst_ref=dst,
            send_sem=send.at[n],
            recv_sem=recv.at[n],
            device_id=at(dx, dy),
            device_id_type=MESH,
        )
        copy.start()
        copies.append(copy)
    for copy in copies:
        copy.wait()
    west_out[...] = west[...]
    east_out[...] = east[...]
    south_out[...] = south[...]
    north_out[...] = north[...]
    corner_out[...] = corner[...]


def edges(packed, south, north, corner):
    shapes = [(GROUPS, RY, 128), (GROUPS, RY, 128), (GROUPS, RX, 128), (GROUPS, RX, 128), (4, 16, 128)]
    return pl.pallas_call(
        edge_kernel,
        out_shape=tuple(jax.ShapeDtypeStruct(s, F32) for s in shapes),
        in_specs=vmem_specs(4),
        out_specs=tuple(vmem_specs(5)),
        scratch_shapes=[pltpu.VMEM(s, F32) for s in shapes]
        + [pltpu.SemaphoreType.DMA((8,)), pltpu.SemaphoreType.DMA((8,))],
        compiler_params=pltpu.CompilerParams(collective_id=1, has_side_effects=True),
        name="edges",
    )(packed, south, north, corner)


def apply_kernel(
    state_ref, packed_ref, west_ref, east_ref, south_ref, north_ref, corner_ref,
    out_ref,
    frame, line, weights, members, results,
):
    a = pl.program_id(0)

    @pl.when(a == 0)
    def build():
        gy = lax.axis_index("gy")
        bottom = gy == 0
        top = gy == NB - 1
        for g in range(GROUPS):
            frame[g, 0, 8:24, :] = west_ref[g]
            frame[g, RX + 1, 8:24, :] = east_ref[g]
            frame[g, 0, 7:8, :] = jnp.where(bottom, west_ref[g, 0:1], corner_ref[0, g : g + 1])
            frame[g, 0, 24:25, :] = jnp.where(top, west_ref[g, RY - 1 : RY], corner_ref[1, g : g + 1])
            frame[g, RX + 1, 7:8, :] = jnp.where(bottom, east_ref[g, 0:1], corner_ref[2, g : g + 1])
            frame[g, RX + 1, 24:25, :] = jnp.where(top, east_ref[g, RY - 1 : RY], corner_ref[3, g : g + 1])
            for p in range(RX):
                r = p * RY
                frame[g, p + 1, 8:24, :] = packed_ref[g, r : r + RY, :]
                frame[g, p + 1, 7:8, :] = jnp.where(
                    bottom, packed_ref[g, r : r + 1, :], south_ref[g, p : p + 1]
                )
                frame[g, p + 1, 24:25, :] = jnp.where(
                    top, packed_ref[g, r + RY - 1 : r + RY, :], north_ref[g, p : p + 1]
                )

    p = lax.div(a, 2)
    odd = lax.rem(a, 2)
    for g in range(GROUPS):
        line[...] = 0.75 * frame[g, p + 1] + 0.25 * frame[g, p + 2 * odd]
        centre = 0.75 * line[8:24, :]
        weights[g * STRIDE : g * STRIDE + 16, :] = centre + 0.25 * line[7:23, :]
        weights[g * STRIDE + 16 : g * STRIDE + 32, :] = centre + 0.25 * line[9:25, :]
    for j in range(M):
        members[j * STRIDE : j * STRIDE + CY, :] = state_ref[j, 0].astype(F32)

    lane = lax.broadcasted_iota(jnp.int32, (16, 128), 1)
    low_side = lane >= M

    for y in range(CY):
        q, par = y // 2, y % 2
        block = members[pl.ds(y, M, stride=STRIDE), :].astype(BF16)
        block = jnp.concatenate([block, block], axis=0)
        value = weights[pl.ds(par * 16 + q, 16, stride=STRIDE), :]
        high = value.astype(BF16).astype(F32)
        low = value - high
        low40 = pltpu.roll(low, 128 - 40, 1)
        parts = [
            jnp.where(low_side, pltpu.roll(low, 40, 1), high),
            jnp.where(low_side, low, pltpu.roll(high, 128 - 40, 1)),
            jnp.where(low_side, low40, pltpu.roll(high, 128 - 80, 1)),
        ]
        left = jnp.concatenate([v.astype(BF16) for v in parts], axis=0)[:, : 2 * M]
        out = jnp.dot(left, block, preferred_element_type=F32)
        results[pl.ds(y, 14, stride=STRIDE), :] = out[0:14]
        results[pl.ds(14 * STRIDE + y, 14, stride=STRIDE), :] = out[16:30]
        results[pl.ds(28 * STRIDE + y, 12, stride=STRIDE), :] = out[32:44]
    for k in range(M):
        out_ref[k, 0] = results[k * STRIDE : k * STRIDE + CY, :].astype(BF16)


def apply(state, packed, west, east, south, north, corner):
    def whole(shape):
        return pl.BlockSpec(shape, lambda a: (0,) * len(shape), pipeline_mode=pl.Buffered(1))

    return pl.pallas_call(
        apply_kernel,
        out_shape=jax.ShapeDtypeStruct((M, CX, CY, 128), BF16),
        grid=(CX,),
        in_specs=[
            pl.BlockSpec((M, 1, CY, 128), lambda a: (0, a, 0, 0)),
            whole((GROUPS, NREG, 128)),
            whole((GROUPS, RY, 128)),
            whole((GROUPS, RY, 128)),
            whole((GROUPS, RX, 128)),
            whole((GROUPS, RX, 128)),
            whole((4, 16, 128)),
        ],
        out_specs=pl.BlockSpec((M, 1, CY, 128), lambda a: (0, a, 0, 0)),
        scratch_shapes=[
            pltpu.VMEM((GROUPS, RX + 2, 32, 128), F32),
            pltpu.VMEM((32, 128), F32),
            pltpu.VMEM((16 * STRIDE, 128), F32),
            pltpu.VMEM((M * STRIDE, 128), F32),
            pltpu.VMEM((M * STRIDE, 128), F32),
        ],
        compiler_params=pltpu.CompilerParams(dimension_semantics=("arbitrary",)),
        name="apply",
    )(state, packed, west, east, south, north, corner)


def per_device(background, obs_perturb, innovation, obs_precision, obs_column, obs_count):
    near, total = exchange(
        obs_perturb[0, 0], innovation[0], obs_precision[0], obs_column[0], obs_count
    )
    packed, south, north, corner = solve(near, total)
    west, east, south, north, corner = edges(packed, south, north, corner)
    return apply(background, packed, west, east, south, north, corner)


def solution(mesh):
    return jax.shard_map(
        per_device,
        mesh=mesh,
        in_specs=(
            P(None, "gx", "gy", None),
            P("gx", "gy", None, None),
            P("gx", "gy", None),
            P("gx", "gy", None),
            P("gx", "gy", None),
            P("gx", "gy"),
        ),
        out_specs=P(None, "gx", "gy", None),
        check_vma=False,
    )
```

time: 183 us -> 58.9 us (0.32); the launches traced: 181 us -> 58.4 us
  Pallas kernels: 0 us -> 57.7 us
  matrix products: 50.1 us -> 0 us
  blocking collectives: 47.3 us -> 0 us
  other arithmetic: 36.2 us -> 0 us
  local copies, waits for them, and re-layouts: 19.8 us -> 0 us
  starting transfers between devices: 18.4 us -> 0 us
  between operations: 4.73 us -> 0.67 us
  waiting for transfers between devices: 4.06 us -> 0 us
    pallas_call x0 -> x4, Pallas kernels: none -> 57.7 us  [the longest x1 20.7 us: exchange(): pl.pallas_call(exchange_kernel, out_shape=(jax.ShapeDtypeStruct((9, ROWS,...]
    dot_general x12 -> x0, matrix products: 50.1 us -> none  [the longest x1 28.8 us: apply_tile(): jnp.einsum('jabl,abjk->kabl', spread, column_transform, precision=lax.Pre...]
    psum x4 -> x0, blocking collectives: 47.3 us -> none  [one_axis_at_a_time(): value = lax.psum(value, axis)]
    sub x42 -> x0, other arithmetic: 18.5 us -> none  [the longest x39 11.6 us: chol_lower(): remain = remain - column[:, None, :] * column[None, :, :]]
    ppermute x8 -> x0, starting transfers between devices: 18.4 us -> none  [the longest x4 14.8 us: with_halo(): lax.ppermute(head, axis, [((i + 1) % count, i) for i in range(count)])]
    reshape x3 -> x0, local copies, waits for them, and re-layouts: 9.25 us -> none  [the longest x1 6.16 us: apply_tile(): column_transform.reshape(cols_east, cols_north, members, members)]
    reduce_sum x4 -> x0, other arithmetic: 5.55 us -> none  [the longest x1 3.43 us: apply_tile(): centre_mean = jnp.mean(float_state, axis=0)]
    mul x53 -> x0, other arithmetic: 4.58 us -> none  [the longest x40 2.79 us: lower_inverse(): remain = remain - factor[:, pivot_id][:, None, :] * row_now[None, :, :]]
  transfers between devices with their start and end apart: 8 -> 0, of which waited for: 4 -> 0; matrix products, arithmetic and copies ran while one was open for 10% -> 0% of each run, Pallas kernels for 0% -> 0%
where the time goes in v1:
time: 58.9 us; the launch traced here: 58.4 us
  Pallas kernels  57.7 us (98%)
  between operations  0.67 us (1%)
    pallas_call x1, Pallas kernels, exchange(): pl.pallas_call(exchange_kernel, out_shape=(jax.ShapeDtypeStruct((9, ROWS,...  20.7 us
    pallas_call x1, Pallas kernels, apply(): pl.pallas_call(apply_kernel, out_shape=jax.ShapeDtypeStruct((M, CX, CY, 1...  15.4 us
    pallas_call x1, Pallas kernels, edges(): pl.pallas_call(edge_kernel, out_shape=tuple((jax.ShapeDtypeStruct(s, F32)...  12.5 us
    pallas_call x1, Pallas kernels, solve(): pl.pallas_call(solve_kernel, out_shape=(jax.ShapeDtypeStruct((GROUPS, NRE...  9.12 us

profile of v1, /device:TPU:1, one launch (start us, length us, event | category | flops | bytes accessed | tf_op | source)
XLA Modules:
  0.0 58.4 jit_solution(864826897992251846)
XLA Ops:
  0.7 20.7 %exchange.1 = (f32[9,48,256]{2,1,0:T(8,128)}, f32[1,128]{1,0:T(1,128)}) custom-call(bf16[40,256]{1,0:T(8,128)(2,1)} %bitcast.4, f32[1,256]{1,0:T(1,128)} %bitcast.5, f32[1,256]{1,0:T(1,128)} %bitcast.6, s32[1,256]{1,0:T(1,128)} %bitcast.7, s32[1,1]{1,0:T(1,128)S(6)} %copy.7.count_ref), custom_call_target="tpu_custom_call" | custom-call | tf_op jit(solution)/shard_map/exchange/pallas_call | solution.py:115
  21.4 9.1 %solve.1 = (f32[14,128,128]{2,1,0:T(8,128)}, f32[14,8,128]{2,1,0:T(8,128)}, f32[14,8,128]{2,1,0:T(8,128)}, f32[4,16,128]{2,1,0:T(8,128)}) custom-call(f32[9,48,256]{2,1,0:T(8,128)} %get-tuple-element.16.near_ref, f32[1,128]{1,0:T(1,128)} %get-tuple-element.17.total_ref), custom_call_target="tpu_custom_call" | custom-call | tf_op jit(solution)/shard_map/solve/pallas_call | solution.py:299
  30.5 12.5 %edges.1 = (f32[14,16,128]{2,1,0:T(8,128)}, f32[14,16,128]{2,1,0:T(8,128)}, f32[14,8,128]{2,1,0:T(8,128)}, f32[14,8,128]{2,1,0:T(8,128)}, f32[4,16,128]{2,1,0:T(8,128)}) custom-call(f32[14,128,128]{2,1,0:T(8,128)} %get-tuple-element.18.packed_ref, f32[14,8,128]{2,1,0:T(8,128)} %get-tuple-element.19.south_ref, f32[14,8,128]{2,1,0:T(8,128)} %get-tuple-element.20.north_ref, ...), custom_call_target="tpu_custom_call" | custom-call | tf_op jit(solution)/shard_map/edges/pallas_call | solution.py:369
  43.0 15.4 %apply.1 = bf16[40,16,32,128]{3,2,1,0:T(8,128)(2,1)} custom-call(bf16[40,16,32,128]{3,2,1,0:T(8,128)(2,1)} %state_ref.1, f32[14,128,128]{2,1,0:T(8,128)} %get-tuple-element.18.packed_ref, f32[14,16,128]{2,1,0:T(8,128)} %get-tuple-element.22.west_ref, f32[14,16,128]{2,1,0:T(8,128)} %get-tuple-element.23.east_ref, f32[14,8,128]{2,1,0:T(8,128)} %get-tuple-element.24.south_ref, ...), custom_call_target="tpu_custom_call" | custom-call | tf_op jit(solution)/shard_map/apply/pallas_call | solution.py:449

commit v2 on v1

v2 whole, which is shorter than its diff:
```python
import functools
import math

import jax
import jax.numpy as jnp
from jax import lax
from jax.experimental import pallas as pl
from jax.experimental.pallas import tpu as pltpu
from jax.sharding import PartitionSpec as P

F32 = jnp.float32
BF16 = jnp.bfloat16
MESH = pl.DeviceIdType.MESH
NB = 16
M = 40
SLOTS = 256
CX, CY = 16, 32
RX, RY = 8, 16
NREG = RX * RY
ROWS = 48
GROUPS = 14
STRIDE = 40
NEIGHBOURS = [(-1, -1), (-1, 0), (-1, 1), (0, -1), (0, 1), (1, -1), (1, 0), (1, 1)]


def vmem_specs(count):
    return [pl.BlockSpec(memory_space=pltpu.VMEM)] * count


BLOCKS = [(ib, jb) for ib in range(5) for jb in range(ib, 5)]


def split(value):
    high = value.astype(BF16)
    return high, (value - high.astype(F32)).astype(BF16)


def analyse_kernel(
    obs_ref, innovation_ref, precision_ref, column_ref, count_ref,
    packed_ref, west_out, east_out, south_out, north_out, corner_out,
    landed, part_a, part_b, slots_a, slots_b,
    table_high, table_low, gram, upper, inverse, flat,
    south_edge, north_edge, corner_edge,
    west_in, east_in, south_in, north_in, corner_in,
    send_near, recv_near, send_a, recv_a, send_b, recv_b, send_edge, recv_edge,
):
    gx = lax.axis_index("gx")
    gy = lax.axis_index("gy")

    def device(dx, dy):
        return (lax.rem(gx + dx + NB, NB), lax.rem(gy + dy + NB, NB))

    barrier = pltpu.get_barrier_semaphore()
    peers = [(0, d) for d in range(1, NB)] + [(d, 0) for d in range(1, NB)]
    peers += [(1, 1), (1, -1), (-1, 1), (-1, -1)]
    for dx, dy in peers:
        pl.semaphore_signal(barrier, inc=1, device_id=device(dx, dy), device_id_type=MESH)

    centered = obs_ref[...].astype(F32)
    centered = centered - jnp.sum(centered, axis=0, keepdims=True) * (1.0 / M)
    innovation = innovation_ref[...]
    slot = lax.broadcasted_iota(jnp.int32, (1, SLOTS), 1)
    weight = jnp.where(slot < count_ref[...], precision_ref[...], 0.0)
    column = column_ref[...]
    east = (gx * CX + lax.shift_right_logical(column, 5)).astype(F32) + 0.5
    north = (gy * CY + jnp.bitwise_and(column, 31)).astype(F32) + 0.5
    mine = landed.at[0]
    mine[0:M, :] = centered
    mine[M : M + 8, :] = jnp.concatenate(
        [innovation, weight, east, north, jnp.zeros((4, SLOTS), F32)], axis=0
    )
    numer = jnp.sum(weight * innovation * innovation, axis=1, keepdims=True)
    squares = jnp.sum(centered * centered, axis=0, keepdims=True)
    denom = jnp.sum(weight * squares, axis=1, keepdims=True) / (M - 1)
    lane = lax.broadcasted_iota(jnp.int32, (1, 128), 1)
    part = jnp.where(lane < 64, numer, denom)
    part_a[...] = part

    pl.semaphore_wait(barrier, len(peers))

    def spread(src, slots, send, recv, along_x):
        copies = []
        for d in range(1, NB):
            copy = pltpu.make_async_remote_copy(
                src_ref=src,
                dst_ref=slots.at[d],
                send_sem=send.at[d],
                recv_sem=recv.at[d],
                device_id=device(d, 0) if along_x else device(0, d),
                device_id_type=MESH,
            )
            copies.append(copy)
        return copies

    first = spread(part_a, slots_a, send_a, recv_a, False)
    for copy in first:
        copy.start()
    near = []
    for n, (dx, dy) in enumerate(NEIGHBOURS):
        copy = pltpu.make_async_remote_copy(
            src_ref=mine,
            dst_ref=landed.at[n + 1],
            send_sem=send_near.at[n],
            recv_sem=recv_near.at[n],
            device_id=device(dx, dy),
            device_id_type=MESH,
        )
        copy.start()
        near.append(copy)
    region = lax.broadcasted_iota(jnp.int32, (NREG, SLOTS), 0)
    centre_east = (gx * CX + 2 * lax.shift_right_logical(region, 4)).astype(F32) + 1.0
    centre_north = (gy * CY + 2 * jnp.bitwise_and(region, 15)).astype(F32) + 1.0
    gram[...] = jnp.zeros_like(gram)
    table_high[...] = jnp.zeros_like(table_high)
    table_low[...] = jnp.zeros_like(table_low)

    def tile(t, carry):
        @pl.when(t == 1)
        def arrive():
            total = part_a[...]
            for copy in first:
                copy.wait()
            for d in range(1, NB):
                total = total + slots_a[d]
            part_b[...] = total
            for copy in spread(part_b, slots_b, send_b, recv_b, True):
                copy.start()
            for copy in near:
                copy.wait()

        obs = landed.at[t]
        east = obs[M + 2 : M + 3, :]
        north = obs[M + 3 : M + 4, :]
        weight = obs[M + 1 : M + 2, :]
        innovation = obs[M : M + 1, :]
        de = east - centre_east + 128.0
        de = jnp.where(de < 0.0, de + 256.0, de)
        de = jnp.where(de >= 256.0, de - 256.0, de) - 128.0
        dn = north - centre_north
        reach = jnp.maximum(1.0 - (de * de + dn * dn) * (1.0 / 256.0), 0.0)
        reach = reach * reach * weight
        reach_high, reach_low = split(reach)
        both = jnp.concatenate([reach_high, reach_low], axis=0)
        for b, (ib, jb) in enumerate(BLOCKS):
            right = obs[8 * jb : 8 * jb + 8, :]
            for ii in range(0, 8, 2):
                i = 8 * ib + ii
                rows = jnp.concatenate(
                    [obs[i : i + 1, :] * right, obs[i + 1 : i + 2, :] * right], axis=0
                )
                high, low = split(rows)
                at = b * 64 + ii * 8
                table_high[at : at + 16, :] = high
                table_low[at : at + 16, :] = low
        pull = jnp.concatenate([obs[0:M, :] * innovation, jnp.zeros((8, SLOTS), F32)], axis=0)
        high, low = split(pull)
        table_high[960:1008, :] = high
        table_low[960:1008, :] = low
        for c in range(0, 1024, 256):
            total = None
            for table in (table_high, table_low):
                out = lax.dot_general(
                    table[c : c + 256, :], both, (((1,), (1,)), ((), ())),
                    preferred_element_type=F32,
                )
                out = out[:, :128] + out[:, 128:]
                total = out if total is None else total + out
            gram[c : c + 256, :] += total
        return carry

    lax.fori_loop(0, 9, tile, 0)

    lane = lax.broadcasted_iota(jnp.int32, (1, 128), 1)
    for copy in spread(part_b, slots_b, send_b, recv_b, True):
        copy.wait()
    both = part_b[...]
    for d in range(1, NB):
        both = both + slots_b[d]
    numer = jnp.sum(jnp.where(lane == 0, both, 0.0), axis=1, keepdims=True)
    denom = jnp.sum(jnp.where(lane == 64, both, 0.0), axis=1, keepdims=True)
    prior = jnp.broadcast_to((M - 1) / (numer / denom), (8, 128))
    sub = lax.broadcasted_iota(jnp.int32, (8, 128), 0)
    inverse[...] = jnp.zeros_like(inverse)
    offset = {pair: 64 * b for b, pair in enumerate(BLOCKS)}

    for ib in range(5):
        cols = list(range(ib, 5))
        state = []
        for t in range(8):
            row = []
            for jb in cols:
                at = offset[(ib, jb)] + 8 * t
                value = gram[at : at + 8, :]
                if jb == ib:
                    value = value + jnp.where(sub == t, prior, 0.0)
                row.append(value)
            row += [jnp.zeros((8, 128), F32)] * ib
            state.append(row)

        def eliminate(p, state):
            base = p * M
            line = [upper[pl.ds(pl.multiple_of(base + 8 * jb, 8), 8), :] for jb in cols]
            line += [inverse[pl.ds(pl.multiple_of(base + 8 * jb, 8), 8), :] for jb in range(ib)]
            new = []
            for t in range(8):
                factor = upper[pl.ds(base + 8 * ib + t, 1), :]
                factor = jnp.broadcast_to(factor, (8, 128))
                new.append([s - factor * v for s, v in zip(state[t], line)])
            return new

        if ib:
            state = lax.fori_loop(0, 8 * ib, eliminate, state, unroll=4)
        state = [
            row + [jnp.where(sub == t, 1.0, 0.0).astype(F32)] for t, row in enumerate(state)
        ]
        for t in range(8):
            scale = lax.rsqrt(jnp.broadcast_to(state[t][0][t : t + 1, :], (8, 128)))
            state[t] = [v * scale for v in state[t]]
            for s in range(t + 1, 8):
                factor = jnp.broadcast_to(state[t][0][s : s + 1, :], (8, 128))
                state[s] = [a - factor * v for a, v in zip(state[s], state[t])]
            p = 8 * ib + t
            for jb, value in zip(cols, state[t][: len(cols)]):
                upper[p * M + 8 * jb : p * M + 8 * jb + 8, :] = value
            for jb, value in enumerate(state[t][len(cols) :]):
                inverse[p * M + 8 * jb : p * M + 8 * jb + 8, :] = value

    pull = [gram[960 + 8 * jb : 968 + 8 * jb, :] for jb in range(5)]
    mean = [jnp.zeros((8, 128), F32)] * 5
    sums = []
    for k in range(M):
        rows = [inverse[k * M + 8 * jb : k * M + 8 * jb + 8, :] for jb in range(k // 8 + 1)]
        inner = rows[0] * pull[0]
        plain = rows[0]
        for jb in range(1, len(rows)):
            inner = inner + rows[jb] * pull[jb]
            plain = plain + rows[jb]
        inner = jnp.broadcast_to(jnp.sum(inner, axis=0, keepdims=True), (8, 128))
        sums.append(jnp.broadcast_to(jnp.sum(plain, axis=0, keepdims=True), (8, 128)))
        for jb in range(len(rows)):
            mean[jb] = mean[jb] + rows[jb] * inner
    mean_sum = mean[0] + mean[1] + mean[2] + mean[3] + mean[4]
    mean_sum = jnp.broadcast_to(jnp.sum(mean_sum, axis=0, keepdims=True), (8, 128))
    root = math.sqrt(M - 1)
    for g in range(GROUPS):
        rows = []
        for part in range(3):
            k = part * GROUPS + g
            if k >= M:
                rows += [jnp.zeros((8, 128), F32)] * 5
                continue
            shift = (1.0 - mean_sum - root * sums[k]) * (1.0 / M)
            for jb in range(5):
                value = mean[jb] + shift
                if jb <= k // 8:
                    value = value + root * inverse[k * M + 8 * jb : k * M + 8 * jb + 8, :]
                rows.append(value)
        rows.append(jnp.zeros((8, 128), F32))
        turned = jnp.transpose(jnp.concatenate(rows, axis=0))
        packed_ref[g] = turned
        flat[g * NREG : (g + 1) * NREG, :] = turned
        south_edge[g] = flat[pl.ds(g * NREG, RX, stride=RY), :]
        north_edge[g] = flat[pl.ds(g * NREG + RY - 1, RX, stride=RY), :]
    flat[GROUPS * NREG : 16 * NREG, :] = jnp.zeros((2 * NREG, 128), F32)
    for c, r in enumerate((0, RY - 1, NREG - RY, NREG - 1)):
        corner_edge[c] = flat[pl.ds(r, 16, stride=NREG), :]

    plan = [
        (packed_ref.at[:, pl.ds(0, RY)], east_in, (-1, 0)),
        (packed_ref.at[:, pl.ds(NREG - RY, RY)], west_in, (1, 0)),
        (south_edge, north_in, (0, -1)),
        (north_edge, south_in, (0, 1)),
        (corner_edge.at[0], corner_in.at[3], (-1, -1)),
        (corner_edge.at[1], corner_in.at[2], (-1, 1)),
        (corner_edge.at[2], corner_in.at[1], (1, -1)),
        (corner_edge.at[3], corner_in.at[0], (1, 1)),
    ]
    copies = []
    for n, (src, dst, (dx, dy)) in enumerate(plan):
        copy = pltpu.make_async_remote_copy(
            src_ref=src,
            dst_ref=dst,
            send_sem=send_edge.at[n],
            recv_sem=recv_edge.at[n],
            device_id=device(dx, dy),
            device_id_type=MESH,
        )
        copy.start()
        copies.append(copy)
    for copy in copies:
        copy.wait()
    west_out[...] = west_in[...]
    east_out[...] = east_in[...]
    south_out[...] = south_in[...]
    north_out[...] = north_in[...]
    corner_out[...] = corner_in[...]


def analyse(obs, innovation, precision, column, count):
    shapes = [(GROUPS, RY, 128), (GROUPS, RY, 128), (GROUPS, RX, 128), (GROUPS, RX, 128), (4, 16, 128)]
    return pl.pallas_call(
        analyse_kernel,
        out_shape=tuple(jax.ShapeDtypeStruct(s, F32) for s in [(GROUPS, NREG, 128)] + shapes),
        in_specs=vmem_specs(5),
        out_specs=tuple(vmem_specs(6)),
        scratch_shapes=[
            pltpu.VMEM((9, ROWS, SLOTS), F32),
            pltpu.VMEM((1, 128), F32),
            pltpu.VMEM((1, 128), F32),
            pltpu.VMEM((NB, 1, 128), F32),
            pltpu.VMEM((NB, 1, 128), F32),
            pltpu.VMEM((1024, SLOTS), BF16),
            pltpu.VMEM((1024, SLOTS), BF16),
            pltpu.VMEM((1024, NREG), F32),
            pltpu.VMEM((M * M, 128), F32),
            pltpu.VMEM((M * M, 128), F32),
            pltpu.VMEM((16 * NREG, 128), F32),
            pltpu.VMEM((GROUPS, RX, 128), F32),
            pltpu.VMEM((GROUPS, RX, 128), F32),
            pltpu.VMEM((4, 16, 128), F32),
        ]
        + [pltpu.VMEM(s, F32) for s in shapes]
        + [
            pltpu.SemaphoreType.DMA((8,)),
            pltpu.SemaphoreType.DMA((8,)),
            pltpu.SemaphoreType.DMA((NB,)),
            pltpu.SemaphoreType.DMA((NB,)),
            pltpu.SemaphoreType.DMA((NB,)),
            pltpu.SemaphoreType.DMA((NB,)),
            pltpu.SemaphoreType.DMA((8,)),
            pltpu.SemaphoreType.DMA((8,)),
        ],
        compiler_params=pltpu.CompilerParams(collective_id=0, has_side_effects=True),
        name="analyse",
    )(obs, innovation, precision, column, count)


def apply_kernel(
    state_ref, packed_ref, west_ref, east_ref, south_ref, north_ref, corner_ref,
    out_ref,
    frame, line, weights, members, results, state, after, read_sem, write_sem,
):
    def reads(a):
        return pltpu.make_async_copy(state_ref.at[:, a], state.at[a], read_sem.at[a])

    def writes(a):
        return pltpu.make_async_copy(after.at[a], out_ref.at[:, a], write_sem.at[a])

    for a in range(CX):
        reads(a).start()

    gy = lax.axis_index("gy")
    bottom = gy == 0
    top = gy == NB - 1
    for g in range(GROUPS):
        frame[g, 0, 8:24, :] = west_ref[g]
        frame[g, RX + 1, 8:24, :] = east_ref[g]
        frame[g, 0, 7:8, :] = jnp.where(bottom, west_ref[g, 0:1], corner_ref[0, g : g + 1])
        frame[g, 0, 24:25, :] = jnp.where(top, west_ref[g, RY - 1 : RY], corner_ref[1, g : g + 1])
        frame[g, RX + 1, 7:8, :] = jnp.where(bottom, east_ref[g, 0:1], corner_ref[2, g : g + 1])
        frame[g, RX + 1, 24:25, :] = jnp.where(top, east_ref[g, RY - 1 : RY], corner_ref[3, g : g + 1])
        for p in range(RX):
            r = p * RY
            frame[g, p + 1, 8:24, :] = packed_ref[g, r : r + RY, :]
            frame[g, p + 1, 7:8, :] = jnp.where(
                bottom, packed_ref[g, r : r + 1, :], south_ref[g, p : p + 1]
            )
            frame[g, p + 1, 24:25, :] = jnp.where(
                top, packed_ref[g, r + RY - 1 : r + RY, :], north_ref[g, p : p + 1]
            )

    def strip(a, carry):
        reads(a).wait()
        p = lax.div(a, 2)
        odd = lax.rem(a, 2)
        for g in range(GROUPS):
            line[...] = 0.75 * frame[g, p + 1] + 0.25 * frame[g, p + 2 * odd]
            centre = 0.75 * line[8:24, :]
            weights[g * STRIDE : g * STRIDE + 16, :] = centre + 0.25 * line[7:23, :]
            weights[g * STRIDE + 16 : g * STRIDE + 32, :] = centre + 0.25 * line[9:25, :]
        for j in range(M):
            members[j * STRIDE : j * STRIDE + CY, :] = state[a, j].astype(F32)

        lane = lax.broadcasted_iota(jnp.int32, (16, 128), 1)
        low_side = lane >= M

        for y in range(CY):
            q, par = y // 2, y % 2
            block = members[pl.ds(y, M, stride=STRIDE), :].astype(BF16)
            block = jnp.concatenate([block, block], axis=0)
            value = weights[pl.ds(par * 16 + q, 16, stride=STRIDE), :]
            high = value.astype(BF16).astype(F32)
            low = value - high
            low40 = pltpu.roll(low, 128 - 40, 1)
            parts = [
                jnp.where(low_side, pltpu.roll(low, 40, 1), high),
                jnp.where(low_side, low, pltpu.roll(high, 128 - 40, 1)),
                jnp.where(low_side, low40, pltpu.roll(high, 128 - 80, 1)),
            ]
            left = jnp.concatenate([v.astype(BF16) for v in parts], axis=0)[:, : 2 * M]
            out = jnp.dot(left, block, preferred_element_type=F32)
            results[pl.ds(y, 14, stride=STRIDE), :] = out[0:14]
            results[pl.ds(14 * STRIDE + y, 14, stride=STRIDE), :] = out[16:30]
            results[pl.ds(28 * STRIDE + y, 12, stride=STRIDE), :] = out[32:44]
        for k in range(M):
            after[a, k] = results[k * STRIDE : k * STRIDE + CY, :].astype(BF16)
        writes(a).start()
        return carry

    lax.fori_loop(0, CX, strip, 0)
    for a in range(CX):
        writes(a).wait()


def apply(state, packed, west, east, south, north, corner):
    return pl.pallas_call(
        apply_kernel,
        out_shape=jax.ShapeDtypeStruct((M, CX, CY, 128), BF16),
        in_specs=[pl.BlockSpec(memory_space=pl.ANY)] + vmem_specs(6),
        out_specs=pl.BlockSpec(memory_space=pl.ANY),
        scratch_shapes=[
            pltpu.VMEM((GROUPS, RX + 2, 32, 128), F32),
            pltpu.VMEM((32, 128), F32),
            pltpu.VMEM((16 * STRIDE, 128), F32),
            pltpu.VMEM((M * STRIDE, 128), F32),
            pltpu.VMEM((M * STRIDE, 128), F32),
            pltpu.VMEM((CX, M, CY, 128), BF16),
            pltpu.VMEM((CX, M, CY, 128), BF16),
            pltpu.SemaphoreType.DMA((CX,)),
            pltpu.SemaphoreType.DMA((CX,)),
        ],
        name="apply",
    )(state, packed, west, east, south, north, corner)


def per_device(background, obs_perturb, innovation, obs_precision, obs_column, obs_count):
    parts = analyse(
        obs_perturb[0, 0], innovation[0], obs_precision[0], obs_column[0], obs_count
    )
    return apply(background, *parts)


def solution(mesh):
    return jax.shard_map(
        per_device,
        mesh=mesh,
        in_specs=(
            P(None, "gx", "gy", None),
            P("gx", "gy", None, None),
            P("gx", "gy", None),
            P("gx", "gy", None),
            P("gx", "gy", None),
            P("gx", "gy"),
        ),
        out_specs=P(None, "gx", "gy", None),
        check_vma=False,
    )
```

time: 58.9 us -> 45.8 us (0.78)
  Pallas kernels: 57.7 us -> 45 us
    pallas_call x3 -> x1, Pallas kernels: 42.3 us -> 32.7 us  [analyse(): pl.pallas_call(analyse_kernel, out_shape=tuple((jax.ShapeDtypeStruct(s, F...]
    pallas_call x1, Pallas kernels: 15.4 us -> 12.3 us  [apply(): pl.pallas_call(apply_kernel, out_shape=jax.ShapeDtypeStruct((M, CX, CY, 1...]
where the time goes in v2:
time: 45.8 us; the launch traced here: 45.7 us
  Pallas kernels  45 us (98%)
  between operations  0.66 us (1%)
    pallas_call x1, Pallas kernels, analyse(): pl.pallas_call(analyse_kernel, out_shape=tuple((jax.ShapeDtypeStruct(s, F...  32.7 us
    pallas_call x1, Pallas kernels, apply(): pl.pallas_call(apply_kernel, out_shape=jax.ShapeDtypeStruct((M, CX, CY, 1...  12.3 us

profile of v2, /device:TPU:1, one launch (start us, length us, event | category | flops | bytes accessed | tf_op | source)
XLA Modules:
  0.0 45.7 jit_solution(6809957817333937564)
XLA Ops:
  0.7 32.7 %analyse.1 = (f32[14,128,128]{2,1,0:T(8,128)}, f32[14,16,128]{2,1,0:T(8,128)}, f32[14,16,128]{2,1,0:T(8,128)}, f32[14,8,128]{2,1,0:T(8,128)}, f32[14,8,128]{2,1,0:T(8,128)}, /*index=5*/f32[4,16,128]{2,1,0:T(8,128)}) custom-call(bf16[40,256]{1,0:T(8,128)(2,1)} %bitcast.4, f32[1,256]{1,0:T(1,128)} %bitcast.5, f32[1,256]{1,0:T(1,128)} %bitcast.6, ...), custom_call_target="tpu_custom_call" | custom-call | tf_op jit(solution)/shard_map/analyse/pallas_call | solution.py:301
  33.3 12.3 %apply.1 = bf16[40,16,32,128]{3,2,1,0:T(8,128)(2,1)} custom-call(bf16[40,16,32,128]{3,2,1,0:T(8,128)(2,1)} %state_ref.1, f32[14,128,128]{2,1,0:T(8,128)} %get-tuple-element.11.packed_ref, f32[14,16,128]{2,1,0:T(8,128)} %get-tuple-element.12.west_ref, f32[14,16,128]{2,1,0:T(8,128)} %get-tuple-element.13.east_ref, f32[14,8,128]{2,1,0:T(8,128)} %get-tuple-element.14.south_ref, ...), custom_call_target="tpu_custom_call" | custom-call | tf_op jit(solution)/shard_map/apply/pallas_call | solution.py:416

commit v3 on v2

--- a/solution.py
+++ b/solution.py
@@ -20,7 +20,7 @@
 ROWS = 48
 GROUPS = 14
 STRIDE = 40
-NEIGHBOURS = [(-1, -1), (-1, 0), (-1, 1), (0, -1), (0, 1), (1, -1), (1, 0), (1, 1)]
+NEIGHBOURS = [(0, -1), (0, 1), (-1, 0), (1, 0), (-1, -1), (-1, 1), (1, -1), (1, 1)]
 
 
 def vmem_specs(count):
@@ -39,7 +39,7 @@
     obs_ref, innovation_ref, precision_ref, column_ref, count_ref,
     packed_ref, west_out, east_out, south_out, north_out, corner_out,
     landed, part_a, part_b, slots_a, slots_b,
-    table_high, table_low, gram, upper, inverse, flat,
+    table, gram, upper, inverse, flat,
     south_edge, north_edge, corner_edge,
     west_in, east_in, south_in, north_in, corner_in,
     send_near, recv_near, send_a, recv_a, send_b, recv_b, send_edge, recv_edge,
@@ -111,12 +111,17 @@
     centre_east = (gx * CX + 2 * lax.shift_right_logical(region, 4)).astype(F32) + 1.0
     centre_north = (gy * CY + 2 * jnp.bitwise_and(region, 15)).astype(F32) + 1.0
     gram[...] = jnp.zeros_like(gram)
-    table_high[...] = jnp.zeros_like(table_high)
-    table_low[...] = jnp.zeros_like(table_low)
+    table[...] = jnp.zeros_like(table)
 
     def tile(t, carry):
-        @pl.when(t == 1)
-        def arrive():
+        for n in range(8):
+
+            @pl.when(t == n + 1)
+            def arrive(copy=near[n]):
+                copy.wait()
+
+        @pl.when(t == 5)
+        def relay():
             total = part_a[...]
             for copy in first:
                 copy.wait()
@@ -125,8 +130,6 @@
             part_b[...] = total
             for copy in spread(part_b, slots_b, send_b, recv_b, True):
                 copy.start()
-            for copy in near:
-                copy.wait()
 
         obs = landed.at[t]
         east = obs[M + 2 : M + 3, :]
@@ -150,22 +153,19 @@
                 )
                 high, low = split(rows)
                 at = b * 64 + ii * 8
-                table_high[at : at + 16, :] = high
-                table_low[at : at + 16, :] = low
+                table[at : at + 16, :SLOTS] = high
+                table[at : at + 16, SLOTS:] = low
         pull = jnp.concatenate([obs[0:M, :] * innovation, jnp.zeros((8, SLOTS), F32)], axis=0)
         high, low = split(pull)
-        table_high[960:1008, :] = high
-        table_low[960:1008, :] = low
+        table[960:1008, :SLOTS] = high
+        table[960:1008, SLOTS:] = low
+        twice = jnp.concatenate([both, both], axis=1)
         for c in range(0, 1024, 256):
-            total = None
-            for table in (table_high, table_low):
-                out = lax.dot_general(
-                    table[c : c + 256, :], both, (((1,), (1,)), ((), ())),
-                    preferred_element_type=F32,
-                )
-                out = out[:, :128] + out[:, 128:]
-                total = out if total is None else total + out
-            gram[c : c + 256, :] += total
+            out = lax.dot_general(
+                table[c : c + 256, :], twice, (((1,), (1,)), ((), ())),
+                preferred_element_type=F32,
+            )
+            gram[c : c + 256, :] += out[:, :128] + out[:, 128:]
         return carry
 
     lax.fori_loop(0, 9, tile, 0)
@@ -257,7 +257,7 @@
                 rows.append(value)
         rows.append(jnp.zeros((8, 128), F32))
         turned = jnp.transpose(jnp.concatenate(rows, axis=0))
-        packed_ref[g] = turned
+        packed_ref[g] = turned.reshape(RX, RY, 128)
         flat[g * NREG : (g + 1) * NREG, :] = turned
         south_edge[g] = flat[pl.ds(g * NREG, RX, stride=RY), :]
         north_edge[g] = flat[pl.ds(g * NREG + RY - 1, RX, stride=RY), :]
@@ -266,8 +266,8 @@
         corner_edge[c] = flat[pl.ds(r, 16, stride=NREG), :]
 
     plan = [
-        (packed_ref.at[:, pl.ds(0, RY)], east_in, (-1, 0)),
-        (packed_ref.at[:, pl.ds(NREG - RY, RY)], west_in, (1, 0)),
+        (packed_ref.at[:, 0], east_in, (-1, 0)),
+        (packed_ref.at[:, RX - 1], west_in, (1, 0)),
         (south_edge, north_in, (0, -1)),
         (north_edge, south_in, (0, 1)),
         (corner_edge.at[0], corner_in.at[3], (-1, -1)),
@@ -300,7 +300,7 @@
     shapes = [(GROUPS, RY, 128), (GROUPS, RY, 128), (GROUPS, RX, 128), (GROUPS, RX, 128), (4, 16, 128)]
     return pl.pallas_call(
         analyse_kernel,
-        out_shape=tuple(jax.ShapeDtypeStruct(s, F32) for s in [(GROUPS, NREG, 128)] + shapes),
+        out_shape=tuple(jax.ShapeDtypeStruct(s, F32) for s in [(GROUPS, RX, RY, 128)] + shapes),
         in_specs=vmem_specs(5),
         out_specs=tuple(vmem_specs(6)),
         scratch_shapes=[
@@ -309,8 +309,7 @@
             pltpu.VMEM((1, 128), F32),
             pltpu.VMEM((NB, 1, 128), F32),
             pltpu.VMEM((NB, 1, 128), F32),
-            pltpu.VMEM((1024, SLOTS), BF16),
-            pltpu.VMEM((1024, SLOTS), BF16),
+            pltpu.VMEM((1024, 2 * SLOTS), BF16),
             pltpu.VMEM((1024, NREG), F32),
             pltpu.VMEM((M * M, 128), F32),
             pltpu.VMEM((M * M, 128), F32),
@@ -338,76 +337,127 @@
 def apply_kernel(
     state_ref, packed_ref, west_ref, east_ref, south_ref, north_ref, corner_ref,
     out_ref,
-    frame, line, weights, members, results, state, after, read_sem, write_sem,
+    frame, south, north, corner, state, after,
+    weights_0, weights_1, members_0, members_1, results_0, results_1,
+    frame_sem, read_sem, write_sem,
 ):
+    weights = (weights_0, weights_1)
+    members = (members_0, members_1)
+    results = (results_0, results_1)
+
     def reads(a):
         return pltpu.make_async_copy(state_ref.at[:, a], state.at[a], read_sem.at[a])
 
     def writes(a):
         return pltpu.make_async_copy(after.at[a], out_ref.at[:, a], write_sem.at[a])
 
-    for a in range(CX):
+    reads(0).start()
+    loads = [
+        (packed_ref, frame.at[:, pl.ds(1, RX), pl.ds(8, RY)]),
+        (west_ref, frame.at[:, 0, pl.ds(8, RY)]),
+        (east_ref, frame.at[:, RX + 1, pl.ds(8, RY)]),
+        (south_ref, south),
+        (north_ref, north),
+        (corner_ref, corner),
+    ]
+    loads = [
+        pltpu.make_async_copy(src, dst, frame_sem.at[n]) for n, (src, dst) in enumerate(loads)
+    ]
+    for copy in loads:
+        copy.start()
+    for a in range(1, CX):
         reads(a).start()
 
+    def take(j, a, half):
+        members[half][j * STRIDE : j * STRIDE + CY, :] = state[a, j].astype(F32)
+
+    def blend(g, p, half):
+        def east(start):
+            near = frame[g, p + 1, start : start + 16, :]
+            far = frame[g, p + 2 * half, start : start + 16, :]
+            return 0.75 * near + 0.25 * far
+
+        centre = 0.75 * east(8)
+        weights[half][g * STRIDE : g * STRIDE + 16, :] = centre + 0.25 * east(7)
+        weights[half][g * STRIDE + 16 : g * STRIDE + 32, :] = centre + 0.25 * east(9)
+
+    def give(k, a, half):
+        after[a, k] = results[half][k * STRIDE : k * STRIDE + CY, :].astype(BF16)
+
+    lane = lax.broadcasted_iota(jnp.int32, (16, 128), 1)
+    low_side = lane >= M
+
+    def column(y, half):
+        q, par = y // 2, y % 2
+        block = members[half][pl.ds(y, M, stride=STRIDE), :].astype(BF16)
+        block = jnp.concatenate([block, block], axis=0)
+        value = weights[half][pl.ds(par * 16 + q, 16, stride=STRIDE), :]
+        high = value.astype(BF16).astype(F32)
+        low = value - high
+        parts = [
+            jnp.where(low_side, pltpu.roll(low, 40, 1), high),
+            jnp.where(low_side, low, pltpu.roll(high, 128 - 40, 1)),
+            jnp.where(low_side, pltpu.roll(low, 128 - 40, 1), pltpu.roll(high, 128 - 80, 1)),
+        ]
+        left = jnp.concatenate([v.astype(BF16) for v in parts], axis=0)[:, : 2 * M]
+        out = jnp.dot(left, block, preferred_element_type=F32)
+        result = results[half]
+        result[pl.ds(y, 14, stride=STRIDE), :] = out[0:14]
+        result[pl.ds(14 * STRIDE + y, 14, stride=STRIDE), :] = out[16:30]
+        result[pl.ds(28 * STRIDE + y, 12, stride=STRIDE), :] = out[32:44]
+
+    reads(0).wait()
+    for j in range(M):
+        take(j, 0, 0)
+    for copy in loads:
+        copy.wait()
     gy = lax.axis_index("gy")
     bottom = gy == 0
     top = gy == NB - 1
     for g in range(GROUPS):
-        frame[g, 0, 8:24, :] = west_ref[g]
-        frame[g, RX + 1, 8:24, :] = east_ref[g]
-        frame[g, 0, 7:8, :] = jnp.where(bottom, west_ref[g, 0:1], corner_ref[0, g : g + 1])
-        frame[g, 0, 24:25, :] = jnp.where(top, west_ref[g, RY - 1 : RY], corner_ref[1, g : g + 1])
-        frame[g, RX + 1, 7:8, :] = jnp.where(bottom, east_ref[g, 0:1], corner_ref[2, g : g + 1])
-        frame[g, RX + 1, 24:25, :] = jnp.where(top, east_ref[g, RY - 1 : RY], corner_ref[3, g : g + 1])
-        for p in range(RX):
-            r = p * RY
-            frame[g, p + 1, 8:24, :] = packed_ref[g, r : r + RY, :]
-            frame[g, p + 1, 7:8, :] = jnp.where(
-                bottom, packed_ref[g, r : r + 1, :], south_ref[g, p : p + 1]
-            )
-            frame[g, p + 1, 24:25, :] = jnp.where(
-                top, packed_ref[g, r + RY - 1 : r + RY, :], north_ref[g, p : p + 1]
-            )
-
-    def strip(a, carry):
-        reads(a).wait()
-        p = lax.div(a, 2)
-        odd = lax.rem(a, 2)
-        for g in range(GROUPS):
-            line[...] = 0.75 * frame[g, p + 1] + 0.25 * frame[g, p + 2 * odd]
-            centre = 0.75 * line[8:24, :]
-            weights[g * STRIDE : g * STRIDE + 16, :] = centre + 0.25 * line[7:23, :]
-            weights[g * STRIDE + 16 : g * STRIDE + 32, :] = centre + 0.25 * line[9:25, :]
-        for j in range(M):
-            members[j * STRIDE : j * STRIDE + CY, :] = state[a, j].astype(F32)
-
-        lane = lax.broadcasted_iota(jnp.int32, (16, 128), 1)
-        low_side = lane >= M
-
-        for y in range(CY):
-            q, par = y // 2, y % 2
-            block = members[pl.ds(y, M, stride=STRIDE), :].astype(BF16)
-            block = jnp.concatenate([block, block], axis=0)
-            value = weights[pl.ds(par * 16 + q, 16, stride=STRIDE), :]
-            high = value.astype(BF16).astype(F32)
-            low = value - high
-            low40 = pltpu.roll(low, 128 - 40, 1)
-            parts = [
-                jnp.where(low_side, pltpu.roll(low, 40, 1), high),
-                jnp.where(low_side, low, pltpu.roll(high, 128 - 40, 1)),
-                jnp.where(low_side, low40, pltpu.roll(high, 128 - 80, 1)),
-            ]
-            left = jnp.concatenate([v.astype(BF16) for v in parts], axis=0)[:, : 2 * M]
-            out = jnp.dot(left, block, preferred_element_type=F32)
-            results[pl.ds(y, 14, stride=STRIDE), :] = out[0:14]
-            results[pl.ds(14 * STRIDE + y, 14, stride=STRIDE), :] = out[16:30]
-            results[pl.ds(28 * STRIDE + y, 12, stride=STRIDE), :] = out[32:44]
-        for k in range(M):
-            after[a, k] = results[k * STRIDE : k * STRIDE + CY, :].astype(BF16)
-        writes(a).start()
+        for p in range(RX + 2):
+            if p == 0:
+                below, above = corner[0, g : g + 1], corner[1, g : g + 1]
+            elif p == RX + 1:
+                below, above = corner[2, g : g + 1], corner[3, g : g + 1]
+            else:
+                below, above = south[g, p - 1 : p], north[g, p - 1 : p]
+            frame[g, p, 7:8, :] = jnp.where(bottom, frame[g, p, 8:9, :], below)
+            frame[g, p, 24:25, :] = jnp.where(top, frame[g, p, 23:24, :], above)
+    for g in range(GROUPS):
+        blend(g, 0, 0)
+
+    def pair(i, carry):
+        for half in range(2):
+            a = 2 * i + half
+            later = jnp.minimum(a + 1, CX - 1)
+            before = jnp.maximum(a - 1, 0)
+
+            @pl.when(a + 1 < CX)
+            def arrive():
+                reads(later).wait()
+
+            jobs = [functools.partial(give, k, before, 1 - half) for k in range(M)]
+            jobs += [functools.partial(blend, g, lax.div(later, 2), 1 - half) for g in range(GROUPS)]
+            jobs += [functools.partial(take, j, later, 1 - half) for j in range(M)]
+            done = 0
+            for y in range(CY):
+                column(y, half)
+                until = (y + 1) * len(jobs) // CY
+                for job in jobs[done:until]:
+                    job()
+                done = until
+
+            @pl.when(a > 0)
+            def leave():
+                writes(before).start()
+
         return carry
 
-    lax.fori_loop(0, CX, strip, 0)
+    lax.fori_loop(0, CX // 2, pair, 0)
+    for k in range(M):
+        give(k, CX - 1, 1)
+    writes(CX - 1).start()
     for a in range(CX):
         writes(a).wait()
 
@@ -416,16 +466,22 @@
     return pl.pallas_call(
         apply_kernel,
         out_shape=jax.ShapeDtypeStruct((M, CX, CY, 128), BF16),
-        in_specs=[pl.BlockSpec(memory_space=pl.ANY)] + vmem_specs(6),
+        in_specs=[pl.BlockSpec(memory_space=pl.ANY)] * 7,
         out_specs=pl.BlockSpec(memory_space=pl.ANY),
         scratch_shapes=[
             pltpu.VMEM((GROUPS, RX + 2, 32, 128), F32),
-            pltpu.VMEM((32, 128), F32),
+            pltpu.VMEM((GROUPS, RX, 128), F32),
+            pltpu.VMEM((GROUPS, RX, 128), F32),
+            pltpu.VMEM((4, 16, 128), F32),
+            pltpu.VMEM((CX, M, CY, 128), BF16),
+            pltpu.VMEM((CX, M, CY, 128), BF16),
+            pltpu.VMEM((16 * STRIDE, 128), F32),
             pltpu.VMEM((16 * STRIDE, 128), F32),
             pltpu.VMEM((M * STRIDE, 128), F32),
             pltpu.VMEM((M * STRIDE, 128), F32),
-            pltpu.VMEM((CX, M, CY, 128), BF16),
-            pltpu.VMEM((CX, M, CY, 128), BF16),
+            pltpu.VMEM((M * STRIDE, 128), F32),
+            pltpu.VMEM((M * STRIDE, 128), F32),
+            pltpu.SemaphoreType.DMA((6,)),
             pltpu.SemaphoreType.DMA((CX,)),
             pltpu.SemaphoreType.DMA((CX,)),
         ],

time: 45.8 us -> 45.3 us (0.989)
  Pallas kernels: 45 us -> 44.5 us
where the time goes in v3:
time: 45.3 us; the launch traced here: 45.1 us
  Pallas kernels  44.5 us (98%)
  between operations  0.66 us (1%)
    pallas_call x1, Pallas kernels, analyse(): pl.pallas_call(analyse_kernel, out_shape=tuple((jax.ShapeDtypeStruct(s, F...  32.2 us
    pallas_call x1, Pallas kernels, apply(): pl.pallas_call(apply_kernel, out_shape=jax.ShapeDtypeStruct((M, CX, CY, 1...  12.2 us

profile of v3, /device:TPU:1, one launch (start us, length us, event | category | flops | bytes accessed | tf_op | source)
XLA Modules:
  0.0 45.1 jit_solution(10922669496883505925)
XLA Ops:
  0.7 32.2 %analyse.1 = (f32[14,8,16,128]{3,2,1,0:T(8,128)}, f32[14,16,128]{2,1,0:T(8,128)}, f32[14,16,128]{2,1,0:T(8,128)}, f32[14,8,128]{2,1,0:T(8,128)}, f32[14,8,128]{2,1,0:T(8,128)}, /*index=5*/f32[4,16,128]{2,1,0:T(8,128)}) custom-call(bf16[40,256]{1,0:T(8,128)(2,1)} %bitcast.4, f32[1,256]{1,0:T(1,128)} %bitcast.5, f32[1,256]{1,0:T(1,128)} %bitcast.6, ...), custom_call_target="tpu_custom_call" | custom-call | tf_op jit(solution)/shard_map/analyse/pallas_call | solution.py:301
  32.9 12.2 %apply.1 = bf16[40,16,32,128]{3,2,1,0:T(8,128)(2,1)} custom-call(bf16[40,16,32,128]{3,2,1,0:T(8,128)(2,1)} %state_ref.1, f32[14,8,16,128]{3,2,1,0:T(8,128)} %get-tuple-element.11.packed_ref, f32[14,16,128]{2,1,0:T(8,128)} %get-tuple-element.12.west_ref, f32[14,16,128]{2,1,0:T(8,128)} %get-tuple-element.13.east_ref, ...), custom_call_target="tpu_custom_call" | custom-call | tf_op jit(solution)/shard_map/apply/pallas_call | solution.py:466

commit v4 on v3

--- a/solution.py
+++ b/solution.py
@@ -19,6 +19,7 @@
 NREG = RX * RY
 ROWS = 48
 GROUPS = 14
+AHEAD = 4
 STRIDE = 40
 NEIGHBOURS = [(0, -1), (0, 1), (-1, 0), (1, 0), (-1, -1), (-1, 1), (1, -1), (1, 1)]
 
@@ -37,12 +38,11 @@
 
 def analyse_kernel(
     obs_ref, innovation_ref, precision_ref, column_ref, count_ref,
-    packed_ref, west_out, east_out, south_out, north_out, corner_out,
+    packed_out, west_in, east_in, south_in, north_in, corner_in,
     landed, part_a, part_b, slots_a, slots_b,
     table, gram, upper, inverse, flat,
-    south_edge, north_edge, corner_edge,
-    west_in, east_in, south_in, north_in, corner_in,
-    send_near, recv_near, send_a, recv_a, send_b, recv_b, send_edge, recv_edge,
+    packed_ref, south_edge, north_edge, corner_edge,
+    send_near, recv_near, send_a, recv_a, send_b, recv_b, send_edge, recv_edge, packed_sem,
 ):
     gx = lax.axis_index("gx")
     gy = lax.axis_index("gy")
@@ -287,13 +287,11 @@
         )
         copy.start()
         copies.append(copy)
+    leave = pltpu.make_async_copy(packed_ref, packed_out, packed_sem)
+    leave.start()
     for copy in copies:
         copy.wait()
-    west_out[...] = west_in[...]
-    east_out[...] = east_in[...]
-    south_out[...] = south_in[...]
-    north_out[...] = north_in[...]
-    corner_out[...] = corner_in[...]
+    leave.wait()
 
 
 def analyse(obs, innovation, precision, column, count):
@@ -302,7 +300,7 @@
         analyse_kernel,
         out_shape=tuple(jax.ShapeDtypeStruct(s, F32) for s in [(GROUPS, RX, RY, 128)] + shapes),
         in_specs=vmem_specs(5),
-        out_specs=tuple(vmem_specs(6)),
+        out_specs=(pl.BlockSpec(memory_space=pl.ANY),) * 6,
         scratch_shapes=[
             pltpu.VMEM((9, ROWS, SLOTS), F32),
             pltpu.VMEM((1, 128), F32),
@@ -314,12 +312,10 @@
             pltpu.VMEM((M * M, 128), F32),
             pltpu.VMEM((M * M, 128), F32),
             pltpu.VMEM((16 * NREG, 128), F32),
+            pltpu.VMEM((GROUPS, RX, RY, 128), F32),
             pltpu.VMEM((GROUPS, RX, 128), F32),
             pltpu.VMEM((GROUPS, RX, 128), F32),
             pltpu.VMEM((4, 16, 128), F32),
-        ]
-        + [pltpu.VMEM(s, F32) for s in shapes]
-        + [
             pltpu.SemaphoreType.DMA((8,)),
             pltpu.SemaphoreType.DMA((8,)),
             pltpu.SemaphoreType.DMA((NB,)),
@@ -328,6 +324,7 @@
             pltpu.SemaphoreType.DMA((NB,)),
             pltpu.SemaphoreType.DMA((8,)),
             pltpu.SemaphoreType.DMA((8,)),
+            pltpu.SemaphoreType.DMA,
         ],
         compiler_params=pltpu.CompilerParams(collective_id=0, has_side_effects=True),
         name="analyse",
@@ -365,7 +362,7 @@
     ]
     for copy in loads:
         copy.start()
-    for a in range(1, CX):
+    for a in range(1, AHEAD):
         reads(a).start()
 
     def take(j, a, half):
@@ -392,14 +389,13 @@
         block = members[half][pl.ds(y, M, stride=STRIDE), :].astype(BF16)
         block = jnp.concatenate([block, block], axis=0)
         value = weights[half][pl.ds(par * 16 + q, 16, stride=STRIDE), :]
-        high = value.astype(BF16).astype(F32)
-        low = value - high
-        parts = [
+        high = value.astype(BF16)
+        low = (value - high.astype(F32)).astype(BF16)
+        left = jnp.concatenate([
             jnp.where(low_side, pltpu.roll(low, 40, 1), high),
             jnp.where(low_side, low, pltpu.roll(high, 128 - 40, 1)),
             jnp.where(low_side, pltpu.roll(low, 128 - 40, 1), pltpu.roll(high, 128 - 80, 1)),
-        ]
-        left = jnp.concatenate([v.astype(BF16) for v in parts], axis=0)[:, : 2 * M]
+        ], axis=0)[:, : 2 * M]
         out = jnp.dot(left, block, preferred_element_type=F32)
         result = results[half]
         result[pl.ds(y, 14, stride=STRIDE), :] = out[0:14]
@@ -436,6 +432,10 @@
             @pl.when(a + 1 < CX)
             def arrive():
                 reads(later).wait()
+
+            @pl.when(a + AHEAD < CX)
+            def ahead():
+                reads(jnp.minimum(a + AHEAD, CX - 1)).start()
 
             jobs = [functools.partial(give, k, before, 1 - half) for k in range(M)]
             jobs += [functools.partial(blend, g, lax.div(later, 2), 1 - half) for g in range(GROUPS)]

time: 45.3 us -> 43 us (0.949)
  Pallas kernels: 44.5 us -> 42.2 us
    pallas_call x1, Pallas kernels: 12.2 us -> 10.9 us  [apply(): pl.pallas_call(apply_kernel, out_shape=jax.ShapeDtypeStruct((M, CX, CY, 1...]
    pallas_call x1, Pallas kernels: 32.2 us -> 31.3 us  [analyse(): pl.pallas_call(analyse_kernel, out_shape=tuple((jax.ShapeDtypeStruct(s, F...]
where the time goes in v4:
time: 43 us; the launch traced here: 42.8 us
  Pallas kernels  42.2 us (98%)
  between operations  0.66 us (2%)
    pallas_call x1, Pallas kernels, analyse(): pl.pallas_call(analyse_kernel, out_shape=tuple((jax.ShapeDtypeStruct(s, F...  31.3 us
    pallas_call x1, Pallas kernels, apply(): pl.pallas_call(apply_kernel, out_shape=jax.ShapeDtypeStruct((M, CX, CY, 1...  10.9 us

profile of v4, /device:TPU:1, one launch (start us, length us, event | category | flops | bytes accessed | tf_op | source)
XLA Modules:
  0.0 42.8 jit_solution(14713827629432250020)
XLA Ops:
  0.7 31.3 %analyse.1 = (f32[14,8,16,128]{3,2,1,0:T(8,128)}, f32[14,16,128]{2,1,0:T(8,128)}, f32[14,16,128]{2,1,0:T(8,128)}, f32[14,8,128]{2,1,0:T(8,128)}, f32[14,8,128]{2,1,0:T(8,128)}, /*index=5*/f32[4,16,128]{2,1,0:T(8,128)}) custom-call(bf16[40,256]{1,0:T(8,128)(2,1)} %bitcast.4, f32[1,256]{1,0:T(1,128)} %bitcast.5, f32[1,256]{1,0:T(1,128)} %bitcast.6, ...), custom_call_target="tpu_custom_call" | custom-call | tf_op jit(solution)/shard_map/analyse/pallas_call | solution.py:299
  32.0 10.9 %apply.1 = bf16[40,16,32,128]{3,2,1,0:T(8,128)(2,1)} custom-call(bf16[40,16,32,128]{3,2,1,0:T(8,128)(2,1)} %state_ref.1, f32[14,8,16,128]{3,2,1,0:T(8,128)} %get-tuple-element.11.packed_ref, f32[14,16,128]{2,1,0:T(8,128)} %get-tuple-element.12.west_ref, f32[14,16,128]{2,1,0:T(8,128)} %get-tuple-element.13.east_ref, ...), custom_call_target="tpu_custom_call" | custom-call | tf_op jit(solution)/shard_map/apply/pallas_call | solution.py:466

commit v5 on v4

--- a/solution.py
+++ b/solution.py
@@ -37,12 +37,13 @@
 
 
 def analyse_kernel(
-    obs_ref, innovation_ref, precision_ref, column_ref, count_ref,
+    obs_in, innovation_in, precision_in, column_in, count_ref,
     packed_out, west_in, east_in, south_in, north_in, corner_in,
+    obs_ref, innovation_ref, precision_ref, column_ref,
     landed, part_a, part_b, slots_a, slots_b,
     table, gram, upper, inverse, flat,
     packed_ref, south_edge, north_edge, corner_edge,
-    send_near, recv_near, send_a, recv_a, send_b, recv_b, send_edge, recv_edge, packed_sem,
+    send_near, recv_near, send_a, recv_a, send_b, recv_b, send_edge, recv_edge, packed_sem, input_sem,
 ):
     gx = lax.axis_index("gx")
     gy = lax.axis_index("gy")
@@ -56,11 +57,27 @@
     for dx, dy in peers:
         pl.semaphore_signal(barrier, inc=1, device_id=device(dx, dy), device_id_type=MESH)
 
+    inputs = [
+        (obs_in, obs_ref),
+        (innovation_in, innovation_ref),
+        (precision_in, precision_ref),
+        (column_in, column_ref),
+    ]
+    inputs = [
+        pltpu.make_async_copy(src, dst, input_sem.at[n]) for n, (src, dst) in enumerate(inputs)
+    ]
+    for copy in inputs:
+        copy.start()
+    gram[...] = jnp.zeros_like(gram)
+    table[...] = jnp.zeros_like(table)
+    inverse[...] = jnp.zeros_like(inverse)
+    for copy in inputs:
+        copy.wait()
     centered = obs_ref[...].astype(F32)
     centered = centered - jnp.sum(centered, axis=0, keepdims=True) * (1.0 / M)
     innovation = innovation_ref[...]
     slot = lax.broadcasted_iota(jnp.int32, (1, SLOTS), 1)
-    weight = jnp.where(slot < count_ref[...], precision_ref[...], 0.0)
+    weight = jnp.where(slot < count_ref[0, 0], precision_ref[...], 0.0)
     column = column_ref[...]
     east = (gx * CX + lax.shift_right_logical(column, 5)).astype(F32) + 0.5
     north = (gy * CY + jnp.bitwise_and(column, 31)).astype(F32) + 0.5
@@ -110,8 +127,6 @@
     region = lax.broadcasted_iota(jnp.int32, (NREG, SLOTS), 0)
     centre_east = (gx * CX + 2 * lax.shift_right_logical(region, 4)).astype(F32) + 1.0
     centre_north = (gy * CY + 2 * jnp.bitwise_and(region, 15)).astype(F32) + 1.0
-    gram[...] = jnp.zeros_like(gram)
-    table[...] = jnp.zeros_like(table)
 
     def tile(t, carry):
         for n in range(8):
@@ -180,7 +195,6 @@
     denom = jnp.sum(jnp.where(lane == 64, both, 0.0), axis=1, keepdims=True)
     prior = jnp.broadcast_to((M - 1) / (numer / denom), (8, 128))
     sub = lax.broadcasted_iota(jnp.int32, (8, 128), 0)
-    inverse[...] = jnp.zeros_like(inverse)
     offset = {pair: 64 * b for b, pair in enumerate(BLOCKS)}
 
     for ib in range(5):
@@ -299,9 +313,13 @@
     return pl.pallas_call(
         analyse_kernel,
         out_shape=tuple(jax.ShapeDtypeStruct(s, F32) for s in [(GROUPS, RX, RY, 128)] + shapes),
-        in_specs=vmem_specs(5),
+        in_specs=[pl.BlockSpec(memory_space=pl.ANY)] * 4 + [pl.BlockSpec(memory_space=pltpu.SMEM)],
         out_specs=(pl.BlockSpec(memory_space=pl.ANY),) * 6,
         scratch_shapes=[
+            pltpu.VMEM((M, SLOTS), BF16),
+            pltpu.VMEM((1, SLOTS), F32),
+            pltpu.VMEM((1, SLOTS), F32),
+            pltpu.VMEM((1, SLOTS), jnp.int32),
             pltpu.VMEM((9, ROWS, SLOTS), F32),
             pltpu.VMEM((1, 128), F32),
             pltpu.VMEM((1, 128), F32),
@@ -325,6 +343,7 @@
             pltpu.SemaphoreType.DMA((8,)),
             pltpu.SemaphoreType.DMA((8,)),
             pltpu.SemaphoreType.DMA,
+            pltpu.SemaphoreType.DMA((4,)),
         ],
         compiler_params=pltpu.CompilerParams(collective_id=0, has_side_effects=True),
         name="analyse",

time: 43 us -> 42.4 us (0.986)
  Pallas kernels: 42.2 us -> 41.6 us
    pallas_call x1, Pallas kernels: 31.3 us -> 30.7 us  [analyse(): pl.pallas_call(analyse_kernel, out_shape=tuple((jax.ShapeDtypeStruct(s, F...]
where the time goes in v5:
time: 42.4 us; the launch traced here: 42.2 us
  Pallas kernels  41.6 us (98%)
  between operations  0.66 us (2%)
    pallas_call x1, Pallas kernels, analyse(): pl.pallas_call(analyse_kernel, out_shape=tuple((jax.ShapeDtypeStruct(s, F...  30.7 us
    pallas_call x1, Pallas kernels, apply(): pl.pallas_call(apply_kernel, out_shape=jax.ShapeDtypeStruct((M, CX, CY, 1...  10.9 us

profile of v5, /device:TPU:1, one launch (start us, length us, event | category | flops | bytes accessed | tf_op | source)
XLA Modules:
  0.0 42.2 jit_solution(5570436303584006752)
XLA Ops:
  0.7 30.7 %analyse.1 = (f32[14,8,16,128]{3,2,1,0:T(8,128)}, f32[14,16,128]{2,1,0:T(8,128)}, f32[14,16,128]{2,1,0:T(8,128)}, f32[14,8,128]{2,1,0:T(8,128)}, f32[14,8,128]{2,1,0:T(8,128)}, /*index=5*/f32[4,16,128]{2,1,0:T(8,128)}) custom-call(bf16[40,256]{1,0:T(8,128)(2,1)} %bitcast.4, f32[1,256]{1,0:T(1,128)} %bitcast.5, f32[1,256]{1,0:T(1,128)} %bitcast.6, ...), custom_call_target="tpu_custom_call" | custom-call | tf_op jit(solution)/shard_map/analyse/pallas_call | solution.py:313
  31.4 10.9 %apply.1 = bf16[40,16,32,128]{3,2,1,0:T(8,128)(2,1)} custom-call(bf16[40,16,32,128]{3,2,1,0:T(8,128)(2,1)} %state_ref.1, f32[14,8,16,128]{3,2,1,0:T(8,128)} %get-tuple-element.11.packed_ref, f32[14,16,128]{2,1,0:T(8,128)} %get-tuple-element.12.west_ref, f32[14,16,128]{2,1,0:T(8,128)} %get-tuple-element.13.east_ref, ...), custom_call_target="tpu_custom_call" | custom-call | tf_op jit(solution)/shard_map/apply/pallas_call | solution.py:485
